TPU v7x, 32 devices: a whole 2x2x4 slice. The times are simulated.
32 devices in a mesh: cell: 8 (over y, x, core), gene: 4 (over z).
Axes of the slice: x: 2, y: 2, z: 4, core: 2. Of those that a mesh axis runs over, the one named last changes fastest.
Arguments:
- counts: int32 [3072, 8192], P('gene', 'cell'), may hold values from 0 to 11
- batch_id: int32 [8192], P('cell'), may hold values from 0 to 63
- live_cells: int32 [8], P('cell'), may hold values from 256 to 1024, as said below
- knot_bin: int32 [8192], P('cell'), may hold values from 0 to 14
- depth_frac: float32 [8192], P('cell'), may hold values from 0 to 1
- cell_covariates: float32 [16, 8192], P(None, 'cell'), may hold values from -3 to 3
- coefficients: float32 [3072, 32], P('gene'), may hold values from -1.2 to 1.2
- batch_effect: float32 [3072, 64], P('gene'), may hold values from -1.8 to 1.8
- factors: bfloat16 [8192, 64], P('cell'), may hold values from -4 to 4
- loadings: bfloat16 [3072, 64], P('gene'), may hold values from -0.19921875 to 0.19921875
Outputs:
- beta_step: float32 [3072, 32], P('gene')
- factor_step: float32 [8192, 64], P('cell')
- loading_score: float32 [3072, 64], P('gene')
Inputs may be any that keep to these rules, and one draw needn't show every extreme that they name: `live_cells`: each index of the cell axis has its live cells in its first slots, at least 256 of them; some index is full in every draw.
All inputs are finite; a program needn't handle non-finite values.
Results may differ from a plain program's by a relative error of at most 0.0003.
Values sent between devices are 32-bit elements; how exact they have to be, the bound alone decides.
A program may use at most 64 MiB of HBM per device.

v0:
```python
import functools

import jax
import jax.numpy as jnp
from jax import lax
from jax.experimental import pallas as pl
from jax.experimental.pallas import tpu as pltpu
from jax.sharding import PartitionSpec as P

GENES = 3072
SPL = 16
BATCHES = 64


ridge_weight = 1.0


def design_rows(knot_bin, depth_frac, cell_covariates):
    levels = jnp.arange(SPL, dtype=jnp.int32)[:, None]
    fraction = depth_frac[None, :]
    hat_basis = jnp.where(levels == knot_bin[None, :], 1.0 - fraction, 0.0)
    hat_basis = hat_basis + jnp.where(levels == knot_bin[None, :] + 1, fraction, 0.0)
    return jnp.concatenate([hat_basis, cell_covariates], axis=0)


def newton_solve(gram_flat, score):
    columns = score.shape[-1]
    identity = jnp.eye(columns, dtype=gram_flat.dtype)
    system = gram_flat.reshape(-1, columns, columns) + ridge_weight * identity
    factor_lower = jnp.linalg.cholesky(system)
    middle = jax.scipy.linalg.solve_triangular(factor_lower, score[..., None], lower=True)
    return jax.scipy.linalg.solve_triangular(factor_lower, middle, lower=True, trans=1)[..., 0]


def local_plain(
    counts,
    batch_id,
    live_cells,
    knot_bin,
    depth_frac,
    cell_covariates,
    coefficients,
    batch_effect,
    factors,
    loadings,
):
    highest = lax.Precision.HIGHEST
    contract = (((1,), (1,)), ((), ()))
    observed = counts.astype(jnp.float32)
    totals = lax.psum(jnp.sum(observed, axis=0), "gene")
    offset = jnp.log((1.0 + totals) / GENES)
    slot_count = observed.shape[1]
    live_mask = (jnp.arange(slot_count, dtype=jnp.int32) < live_cells[0]).astype(jnp.float32)
    design = design_rows(knot_bin, depth_frac, cell_covariates)
    columns = design.shape[0]
    onehot = (jnp.arange(BATCHES, dtype=jnp.int32)[:, None] == batch_id[None, :]).astype(
        jnp.float32
    )
    stacked = jnp.concatenate([design, onehot], axis=0)
    linear = jnp.dot(
        jnp.concatenate([coefficients, batch_effect], axis=1), stacked, precision=highest
    )
    latent = lax.dot_general(loadings, factors, contract, preferred_element_type=jnp.float32)
    linear_pred = offset[None, :] + linear + latent
    expected = jnp.exp(linear_pred)
    weight = expected * live_mask
    residual = (observed - expected) * live_mask
    pairs = (design[:, None, :] * design[None, :, :]).reshape(columns * columns, slot_count)
    gram_part = lax.dot_general(weight, pairs, contract, precision=highest)
    score_part = lax.dot_general(residual, design, contract, precision=highest)
    gram_share, score_share = (
        lax.psum_scatter(gram_part, "cell", scatter_dimension=0, tiled=True),
        lax.psum_scatter(score_part, "cell", scatter_dimension=0, tiled=True),
    )
    step_share = newton_solve(gram_share, score_share)
    beta_step = lax.all_gather(step_share, "cell", axis=0, tiled=True)
    expected_next = jnp.exp(linear_pred + jnp.dot(beta_step, design, precision=highest))
    weight_next = expected_next * live_mask
    residual_next = (observed - expected_next) * live_mask
    factors_wide = factors.astype(jnp.float32)
    loads_wide = loadings.astype(jnp.float32)
    grad_load = jnp.dot(residual_next, factors_wide, precision=highest)
    curv_load = jnp.dot(weight_next, factors_wide * factors_wide, precision=highest)
    back = (((0,), (0,)), ((), ()))
    grad_fact = lax.dot_general(residual_next, loads_wide, back, precision=highest)
    curv_fact = lax.dot_general(weight_next, loads_wide * loads_wide, back, precision=highest)
    grad_load, curv_load = lax.psum((grad_load, curv_load), "cell")
    grad_fact, curv_fact = lax.psum((grad_fact, curv_fact), "gene")
    factor_step = grad_fact / (curv_fact + 1.0)
    loading_score = grad_load / jnp.sqrt(curv_load + 1.0)
    return (beta_step, factor_step, loading_score)


MESH = pl.DeviceIdType.MESH
F32, BF16 = jnp.float32, jnp.bfloat16
VM = pl.BlockSpec(memory_space=pltpu.VMEM)
ROWS_BY_ROWS = (((1,), (1,)), ((), ()))
ACROSS = (((1,), (0,)), ((), ()))
DOWN = (((0,), (0,)), ((), ()))
LIMIT = 60 * 1024 * 1024


def split(x):
    high = x.astype(BF16)
    return high, (x - high.astype(F32)).astype(BF16)


def mul(a, b, dims):
    return lax.dot_general(a, b, dims, preferred_element_type=F32)


def remote(src, dst, send, recv, where):
    return pltpu.make_async_remote_copy(
        src_ref=src, dst_ref=dst, send_sem=send, recv_sem=recv, device_id=where, device_id_type=MESH
    )


def meet(groups):
    barrier = pltpu.get_barrier_semaphore()
    count = 0
    for axis, n in groups:
        me = lax.axis_index(axis)
        for d in range(1, n):
            pl.semaphore_signal(
                barrier, inc=1, device_id={axis: lax.rem(me + d, n)}, device_id_type=MESH
            )
        count += n - 1
    pl.semaphore_wait(barrier, count)


def totals_kernel(n, x_ref, o_ref, recv, send_sem, recv_sem):
    me = lax.axis_index("gene")
    meet((("gene", n),))
    copies = []
    for d in range(1, n):
        copies.append(
            remote(
                x_ref, recv.at[d - 1], send_sem.at[d - 1], recv_sem.at[d - 1],
                {"gene": lax.rem(me + d, n)},
            )
        )
        copies[-1].start()
    total = x_ref[...]
    for d in range(1, n):
        copies[d - 1].wait()
        total = total + recv[d - 1]
    o_ref[...] = total


def design_of(knot_ref, frac_ref, cov_ref):
    slots = knot_ref.shape[1]
    levels = lax.broadcasted_iota(jnp.int32, (SPL, slots), 0)
    knot, frac = knot_ref[...], frac_ref[...]
    hats = jnp.where(levels == knot, 1.0 - frac, 0.0)
    hats = hats + jnp.where(levels == knot + 1, frac, 0.0)
    return hats, cov_ref[...]


def first_kernel(
    counts_ref, totals_ref, batch_ref, live_ref, knot_ref, frac_ref, cov_ref, coef_ref, shift_ref,
    factors_ref, loads_ref, g_ref, lin_ref, rhs, pair_hi, pair_lo, des_hi, des_lo, extra,
):
    slots = counts_ref.shape[1]

    @pl.when(pl.program_id(0) == 0)
    def _():
        hats, cov = design_of(knot_ref, frac_ref, cov_ref)
        ncov = cov.shape[0]
        half = ncov // 2
        design_hi, design_lo = split(jnp.concatenate([hats, cov], axis=0))
        hot = lax.broadcasted_iota(jnp.int32, (BATCHES, slots), 0) == batch_ref[...]
        hot = jnp.where(hot, 1.0, 0.0).astype(BF16)
        width = SPL + ncov
        rhs[0:width] = design_hi
        rhs[width : 2 * width] = design_hi
        rhs[2 * width : 3 * width] = design_lo
        rhs[3 * width : 3 * width + BATCHES] = hot
        rhs[3 * width + BATCHES : 3 * width + 2 * BATCHES] = hot
        rhs[3 * width + 2 * BATCHES :] = factors_ref[...]

        def put(at, block):
            high, low = split(block)
            pair_hi[at : at + block.shape[0]] = high
            pair_lo[at : at + block.shape[0]] = low

        at = 0
        for p in range(SPL):
            put(at, hats[p : p + 1] * cov)
            at += ncov
        for i in range(half):
            put(at, cov[i : i + 1] * cov)
            at += ncov
        for i in range(half, ncov, 2):
            put(
                at,
                jnp.concatenate(
                    [cov[i : i + 1] * cov[half:], cov[i + 1 : i + 2] * cov[half:]], axis=0
                ),
            )
            at += ncov
        put(at, hats * hats)
        at += SPL
        later = jnp.concatenate([hats[1:], jnp.zeros((1, slots), F32)], axis=0)
        put(at, hats * later)
        at += SPL
        put(at, jnp.zeros((width, slots), F32))
        des_hi[...] = jnp.zeros(des_hi.shape, BF16)
        des_lo[...] = jnp.zeros(des_lo.shape, BF16)
        des_hi[128 - width : 128] = design_hi
        des_lo[128 - width : 128] = design_lo
        extra[0:1] = jnp.log((1.0 + totals_ref[...]) / GENES)
        places = lax.broadcasted_iota(jnp.int32, (1, slots), 1)
        extra[1:2] = jnp.where(places < live_ref[0], 1.0, 0.0)

    coef_hi, coef_lo = split(coef_ref[...])
    shift_hi, shift_lo = split(shift_ref[...])
    lhs = jnp.concatenate([coef_hi, coef_lo, coef_hi, shift_hi, shift_lo, loads_ref[...]], axis=0)
    linear = mul(lhs, rhs[...], DOWN) + extra[0:1]
    lin_ref[...] = linear
    mask = extra[1:2]
    expected = jnp.exp(linear)
    w_hi, w_lo = split(expected * mask)
    r_hi, r_lo = split((counts_ref[...].astype(F32) - expected) * mask)
    gram = mul(w_hi, pair_hi[...], ROWS_BY_ROWS)
    gram = gram + mul(w_hi, pair_lo[...], ROWS_BY_ROWS)
    gram = gram + mul(w_lo, pair_hi[...], ROWS_BY_ROWS)
    score = mul(r_hi, des_hi[...], ROWS_BY_ROWS)
    score = score + mul(r_hi, des_lo[...], ROWS_BY_ROWS)
    score = score + mul(r_lo, des_hi[...], ROWS_BY_ROWS)
    blocks, rows, wide = g_ref.shape
    g_ref[:, :, : wide - 128] = gram[:, : wide - 128].reshape(blocks, rows, wide - 128)
    g_ref[:, :, wide - 128 :] = (gram[:, wide - 128 :] + score).reshape(blocks, rows, 128)


def solve(g, x):
    half = SPL // 2
    cov_at, low_at, hat_at = SPL * SPL, SPL * SPL + half * SPL, SPL * SPL + half * SPL + half * half
    off_at, score_at = hat_at + SPL, hat_at + 2 * SPL
    spot = lax.broadcasted_iota(jnp.int32, (half, g.shape[1]), 0)

    def one(block, i):
        return block[i : i + 1]

    lo = {}
    hi = {}
    for i in range(SPL):
        unit = jnp.where(spot == i % half, ridge_weight, 0.0)
        if i < half:
            lo[i] = g[cov_at + i * SPL : cov_at + i * SPL + half] + unit
            hi[i] = g[cov_at + i * SPL + half : cov_at + (i + 1) * SPL]
        else:
            hi[i] = g[low_at + (i - half) * half : low_at + (i - half + 1) * half] + unit
    b_lo = g[score_at + SPL : score_at + SPL + half]
    b_hi = g[score_at + SPL + half : score_at + 2 * SPL]
    pivot_inv, edge, side_lo, side_hi, rest = [], [], [], [], []
    for p in range(SPL):
        d = g[hat_at + p : hat_at + p + 1] + ridge_weight
        u_lo = g[p * SPL : p * SPL + half]
        u_hi = g[p * SPL + half : (p + 1) * SPL]
        b = g[score_at + p : score_at + p + 1]
        if p > 0:
            ratio = edge[-1] * pivot_inv[-1]
            d = d - ratio * edge[-1]
            u_lo = u_lo - ratio * side_lo[-1]
            u_hi = u_hi - ratio * side_hi[-1]
            b = b - ratio * rest[-1]
        inv = 1.0 / d
        pivot_inv.append(inv)
        edge.append(g[off_at + p : off_at + p + 1])
        side_lo.append(u_lo)
        side_hi.append(u_hi)
        rest.append(b)
        scaled_lo, scaled_hi = u_lo * inv, u_hi * inv
        b_lo = b_lo - scaled_lo * b
        b_hi = b_hi - scaled_hi * b
        for i in range(SPL):
            if i < half:
                f = one(scaled_lo, i)
                lo[i] = lo[i] - f * u_lo
            else:
                f = one(scaled_hi, i - half)
            hi[i] = hi[i] - f * u_hi
    c_inv, c_rest = [], []
    for j in range(SPL):
        if j < half:
            inv = 1.0 / one(lo[j], j)
            b = one(b_lo, j)
            s_lo = lo[j] * inv
            b_lo = b_lo - s_lo * b
        else:
            inv = 1.0 / one(hi[j], j - half)
            b = one(b_hi, j - half)
        s_hi = hi[j] * inv
        b_hi = b_hi - s_hi * b
        c_inv.append(inv)
        c_rest.append(b)
        for i in range(j + 1, SPL):
            if i < half:
                f = one(s_lo, i)
                lo[i] = lo[i] - f * lo[j]
            else:
                f = one(s_hi, i - half)
            hi[i] = hi[i] - f * hi[j]
    for j in reversed(range(SPL)):
        found = c_rest[j] * c_inv[j]
        x[SPL + j : SPL + j + 1] = found
        for i in range(j):
            c_rest[i] = c_rest[i] - (one(hi[i], j - half) if j >= half else one(lo[i], j)) * found
    x_lo, x_hi = x[SPL : SPL + half], x[SPL + half : 2 * SPL]
    after = None
    for p in reversed(range(SPL)):
        gone = jnp.sum(side_lo[p] * x_lo + side_hi[p] * x_hi, axis=0, keepdims=True)
        b = rest[p] - gone
        if after is not None:
            b = b - edge[p] * after
        after = b * pivot_inv[p]
        x[p : p + 1] = after


def newton_kernel(
    n, g_ref, o_ref, from_pair, to_far, from_far, tall, turned, mine, theirs,
    pair_send, pair_recv, far_send, far_recv, out_send, out_recv,
):
    me = lax.axis_index("cell")
    core, chip = lax.rem(me, 2), me // 2
    chips, rows, wide = n // 2, g_ref.shape[1], g_ref.shape[2]
    meet((("cell", n),))
    pair = []
    for d in list(range(1, chips)) + [0]:
        k = lax.rem(chip + d, chips)
        pair.append(
            remote(
                g_ref.at[2 * k + 1 - core], from_pair.at[d], pair_send.at[d], pair_recv.at[d],
                {"cell": me + 1 - 2 * core},
            )
        )
        pair[-1].start()
    far = []
    for d in range(1, chips):
        k = lax.rem(chip + d, chips)
        pair[d - 1].wait()
        to_far[d - 1] = g_ref[2 * k + core] + from_pair[d]
        far.append(
            remote(
                to_far.at[d - 1], from_far.at[d - 1], far_send.at[d - 1], far_recv.at[d - 1],
                {"cell": 2 * k + core},
            )
        )
        far[-1].start()
    pair[chips - 1].wait()
    total = g_ref[me] + from_pair[0]
    for d in range(1, chips):
        far[d - 1].wait()
        total = total + from_far[d - 1]
    tall[0:rows] = total
    if rows < 128:
        tall[rows:128] = jnp.zeros((128 - rows, wide), F32)
    turned[...] = tall[...].T
    solve(turned, mine)
    out = []
    for d in range(1, n):
        out.append(
            remote(
                mine, theirs.at[d - 1], out_send.at[d - 1], out_recv.at[d - 1],
                {"cell": lax.rem(me + d, n)},
            )
        )
        out[-1].start()
    width = mine.shape[0]
    fill = jnp.zeros((128 - width, 128), F32)

    def put(owner, block):
        o_ref[owner] = jnp.concatenate([block, fill], axis=0).T[:rows, :width]

    put(me, mine[...])
    for d in range(1, n):
        out[d - 1].wait()
        put(lax.rem(me + n - d, n), theirs[d - 1])


def spread(block):
    wide = block.astype(F32)
    zero = jnp.zeros(wide.shape, F32)
    square_hi, square_lo = split(jnp.concatenate([zero, wide * wide], axis=0))
    return jnp.concatenate([wide, zero], axis=0).astype(BF16), square_hi, square_lo


def last_kernel(
    n, m, counts_ref, lin_ref, live_ref, knot_ref, frac_ref, cov_ref, beta_ref, factors_ref,
    loads_ref, ls_ref, fs_ref, rhs, mask_ref, f_one, f_hi, f_lo, gl_ref, gf_ref,
    from_c, my_l, their_l, from_g, my_f, their_f,
    c_send, c_recv, g_send, g_recv, l_send, l_recv, f_send, f_recv,
):
    cell, gene = lax.axis_index("cell"), lax.axis_index("gene")
    half = gl_ref.shape[2] // 2
    span = gf_ref.shape[2]
    slots = counts_ref.shape[1]
    hats, cov = design_of(knot_ref, frac_ref, cov_ref)
    design_hi, design_lo = split(jnp.concatenate([hats, cov], axis=0))
    width = design_hi.shape[0]
    rhs[0:width] = design_hi
    rhs[width : 2 * width] = design_hi
    rhs[2 * width : 3 * width] = design_lo
    places = lax.broadcasted_iota(jnp.int32, (1, slots), 1)
    mask_ref[0:1] = jnp.where(places < live_ref[...], 1.0, 0.0)
    f_one[...], f_hi[...], f_lo[...] = spread(factors_ref[...])
    blocks, rows, _ = beta_ref.shape
    beta_hi, beta_lo = split(beta_ref[...].reshape(blocks * rows, width))
    lhs = jnp.concatenate([beta_hi, beta_lo, beta_hi], axis=1)
    l_one, l_hi, l_lo = spread(loads_ref[...])
    meet((("cell", n), ("gene", m)))
    across, along = [], []
    for d in list(range(1, m)) + [0]:
        to = lax.rem(gene + d, m)
        cols = pl.ds(pl.multiple_of(to * span, span), span)
        delta = mul(lhs, rhs[:, cols], ACROSS)
        mask = mask_ref[0:1, cols]
        expected = jnp.exp(lin_ref[:, cols] + delta)
        w_hi, w_lo = split(expected * mask)
        r_hi, r_lo = split((counts_ref[:, cols].astype(F32) - expected) * mask)
        gf = mul(l_one, r_hi, ACROSS) + mul(l_one, r_lo, ACROSS)
        gf = gf + mul(l_hi, w_hi, ACROSS) + mul(l_lo, w_hi, ACROSS) + mul(l_hi, w_lo, ACROSS)
        gf_ref[d] = gf
        if d > 0:
            along.append(
                remote(
                    gf_ref.at[d], from_g.at[d - 1], g_send.at[d - 1], g_recv.at[d - 1],
                    {"gene": to},
                )
            )
            along[-1].start()
        one, high, low = f_one[:, cols], f_hi[:, cols], f_lo[:, cols]
        gl = mul(r_hi, one, ROWS_BY_ROWS) + mul(r_lo, one, ROWS_BY_ROWS)
        gl = gl + mul(w_hi, high, ROWS_BY_ROWS)
        gl = gl + mul(w_hi, low, ROWS_BY_ROWS) + mul(w_lo, high, ROWS_BY_ROWS)
        gl = gl.reshape(gl_ref.shape)
        if d == 1:
            gl_ref[...] = gl
        else:
            gl_ref[...] += gl
    for d in range(1, n):
        to = lax.rem(cell + d, n)
        across.append(
            remote(gl_ref.at[to], from_c.at[d - 1], c_send.at[d - 1], c_recv.at[d - 1], {"cell": to})
        )
        across[-1].start()
    total = gl_ref[cell]
    for d in range(1, n):
        across[d - 1].wait()
        total = total + from_c[d - 1]
    my_l[...] = total[:, :half] / jnp.sqrt(total[:, half:] + 1.0)
    their_l[cell] = my_l[...]
    out_l, out_f = [], []
    for d in range(1, n):
        out_l.append(
            remote(
                my_l, their_l.at[cell], l_send.at[d - 1], l_recv.at[d - 1],
                {"cell": lax.rem(cell + d, n)},
            )
        )
        out_l[-1].start()
    total = gf_ref[0]
    for d in range(1, m):
        along[d - 1].wait()
        total = total + from_g[d - 1]
    my_f[...] = total[:half] / (total[half:] + 1.0)
    for d in range(1, m):
        out_f.append(
            remote(
                my_f, their_f.at[d - 1], f_send.at[d - 1], f_recv.at[d - 1],
                {"gene": lax.rem(gene + d, m)},
            )
        )
        out_f[-1].start()
    def put(owner, block):
        fs_ref[:, pl.ds(pl.multiple_of(owner * span, span), span)] = block

    put(gene, my_f[...])
    for d in range(1, n):
        out_l[d - 1].wait()
    found = their_l[...].reshape(ls_ref.shape[1], half)
    ls_ref[...] = jnp.concatenate([found, jnp.zeros(found.shape, F32)], axis=1).T[:half]
    for d in range(1, m):
        out_f[d - 1].wait()
        put(lax.rem(gene + m - d, m), their_f[d - 1])


def local_fused(
    n, m, counts, batch_id, live_cells, knot_bin, depth_frac, cell_covariates, coefficients,
    batch_effect, factors, loadings,
):
    genes, slots = counts.shape
    rows, span, latent = genes // n, slots // m, factors.shape[1]
    ncov = cell_covariates.shape[0]
    width = SPL + ncov
    wide = SPL * ncov + ncov * ncov * 3 // 4 + 2 * SPL + width
    steps = 2
    tile, blocks = genes // steps, n // steps
    dma = pltpu.SemaphoreType.DMA
    shape = jax.ShapeDtypeStruct

    def params(**kw):
        return pltpu.CompilerParams(vmem_limit_bytes=LIMIT, **kw)

    part = jnp.sum(counts, axis=0, keepdims=True).astype(F32)
    totals = pl.pallas_call(
        functools.partial(totals_kernel, m),
        out_shape=shape((1, slots), F32),
        in_specs=[VM],
        out_specs=VM,
        scratch_shapes=[pltpu.VMEM((m - 1, 1, slots), F32), dma((m - 1,)), dma((m - 1,))],
        compiler_params=params(collective_id=0, has_side_effects=True),
        name="totals",
    )(part)

    def by_rows(*tail):
        return pl.BlockSpec((tile,) + tail, lambda i: (i,) + (0,) * len(tail))

    def by_lanes(count):
        return pl.BlockSpec((count, tile), lambda i: (0, i))

    def by_blocks(*tail):
        return pl.BlockSpec((blocks,) + tail, lambda i: (i,) + (0,) * len(tail))

    def whole(*dims):
        return pl.BlockSpec(dims, lambda i: (0,) * len(dims))

    smem = pl.BlockSpec(memory_space=pltpu.SMEM)
    knot, frac, batch = (v.reshape(1, slots) for v in (knot_bin, depth_frac, batch_id))
    line = whole(1, slots)
    gram, lin = pl.pallas_call(
        first_kernel,
        grid=(steps,),
        out_shape=(shape((n, rows, wide), F32), shape((genes, slots), F32)),
        in_specs=[
            by_rows(slots), line, line, smem, line, line, whole(ncov, slots),
            by_lanes(width), by_lanes(BATCHES), whole(latent, slots), by_lanes(latent),
        ],
        out_specs=(by_blocks(rows, wide), by_rows(slots)),
        scratch_shapes=[
            pltpu.VMEM((3 * width + 2 * BATCHES + latent, slots), BF16),
            pltpu.VMEM((wide, slots), BF16),
            pltpu.VMEM((wide, slots), BF16),
            pltpu.VMEM((128, slots), BF16),
            pltpu.VMEM((128, slots), BF16),
            pltpu.VMEM((8, slots), F32),
        ],
        compiler_params=params(),
        name="first",
    )(
        counts, totals, batch, live_cells, knot, frac, cell_covariates, coefficients.T,
        batch_effect.T, factors.T, loadings.T,
    )
    chips = n // 2
    beta = pl.pallas_call(
        functools.partial(newton_kernel, n),
        out_shape=shape((n, rows, width), F32),
        in_specs=[VM],
        out_specs=VM,
        scratch_shapes=[
            pltpu.VMEM((chips, rows, wide), F32),
            pltpu.VMEM((chips - 1, rows, wide), F32),
            pltpu.VMEM((chips - 1, rows, wide), F32),
            pltpu.VMEM((128, wide), F32),
            pltpu.VMEM((wide, 128), F32),
            pltpu.VMEM((width, 128), F32),
            pltpu.VMEM((n - 1, width, 128), F32),
            dma((chips,)), dma((chips,)), dma((chips - 1,)), dma((chips - 1,)),
            dma((n - 1,)), dma((n - 1,)),
        ],
        compiler_params=params(collective_id=1, has_side_effects=True),
        name="newton",
    )(gram)
    ls, fs = pl.pallas_call(
        functools.partial(last_kernel, n, m),
        out_shape=(shape((latent, genes), F32), shape((latent, slots), F32)),
        in_specs=[VM] * 9,
        out_specs=(VM, VM),
        scratch_shapes=[
            pltpu.VMEM((3 * width, slots), BF16),
            pltpu.VMEM((8, slots), F32),
            pltpu.VMEM((2 * latent, slots), BF16),
            pltpu.VMEM((2 * latent, slots), BF16),
            pltpu.VMEM((2 * latent, slots), BF16),
            pltpu.VMEM((n, rows, 2 * latent), F32),
            pltpu.VMEM((m, 2 * latent, span), F32),
            pltpu.VMEM((n - 1, rows, 2 * latent), F32),
            pltpu.VMEM((rows, latent), F32),
            pltpu.VMEM((n, rows, latent), F32),
            pltpu.VMEM((m - 1, 2 * latent, span), F32),
            pltpu.VMEM((latent, span), F32),
            pltpu.VMEM((m - 1, latent, span), F32),
            dma((n - 1,)), dma((n - 1,)), dma((m - 1,)), dma((m - 1,)),
            dma((n - 1,)), dma((n - 1,)), dma((m - 1,)), dma((m - 1,)),
        ],
        compiler_params=params(collective_id=2, has_side_effects=True),
        name="last",
    )(
        counts, lin, live_cells.reshape(1, 1), knot, frac, cell_covariates, beta,
        factors.T, loadings.T,
    )
    return beta.reshape(genes, width), fs.T, ls.T


def local(n, m, *args):
    counts, cov, factors = args[0], args[5], args[8]
    genes, slots = counts.shape
    fits = (
        n % 2 == 0
        and n > 2
        and m > 1
        and genes % (16 * n) == 0
        and genes // n <= 128
        and slots % (128 * m) == 0
        and cov.shape[0] == SPL
        and factors.shape[1] == 64
    )
    if fits:
        return local_fused(n, m, *args)
    return local_plain(*args)


def solution(mesh):
    placed = (
        P("gene", "cell"),
        P("cell"),
        P("cell"),
        P("cell"),
        P("cell"),
        P(None, "cell"),
        P("gene", None),
        P("gene", None),
        P("cell", None),
        P("gene", None),
    )
    return jax.shard_map(
        functools.partial(local, mesh.shape["cell"], mesh.shape["gene"]),
        mesh=mesh,
        in_specs=placed,
        out_specs=(P("gene", None), P("cell", None), P("gene", None)),
        check_vma=False,
    )
```

profile of v0, /device:TPU:0, one launch (start us, length us, event | category | flops | bytes accessed | tf_op | source)
XLA Modules:
  0.0 73.5 jit_solution(3249578162455704482)
XLA Ops:
  1.3 2.1 %reduce_sum.9 = s32[1024]{0:T(1024)S(1)} reduce(s32[768,1024]{1,0:T(8,128)} %counts_ref.3, s32[]{:T(128)} %constant.0.clone.1), dimensions={0}, to_apply=%region_0.0 | reduce | flops 785408 | bytes 3149828 | tf_op jit(solution)/shard_map/reduce_sum | solution.py:505
  3.4 0.6 convert_element_type.5
  4.0 8.6 %totals.1.totals_ref = f32[1,1024]{1,0:T(1,128)} custom-call(f32[1,1024]{1,0:T(1,128)} %bitcast.22), custom_call_target="tpu_custom_call" | custom-call | tf_op jit(solution)/shard_map/totals/pallas_call | solution.py:506
  12.6 8.9 %first.1 = (f32[8,96,512]{2,1,0:T(8,128)}, f32[768,1024]{1,0:T(8,128)}) custom-call(s32[768,1024]{1,0:T(8,128)} %counts_ref.3, f32[1,1024]{1,0:T(1,128)} %totals.1.totals_ref, s32[1,1024]{1,0:T(1,128)} %bitcast.27, s32[1]{0:T(128)} %copy.16.live_ref, s32[1,1024]{1,0:T(1,128)} %bitcast.23, f32[1,1024]{1,0:T(1,128)} %bitcast.25, f32[16,1024]{1,0:T(8,128)} %cov_ref.3, ...), custom_call_target="tpu_custom_call" | custom-call | tf_op jit(solution)/shard_map/first/pallas_call | solution.py:531
  21.5 21.4 %newton.1.beta_ref = f32[8,96,32]{2,1,0:T(8,128)} custom-call(f32[8,96,512]{2,1,0:T(8,128)} %get-tuple-element.7.g_ref), custom_call_target="tpu_custom_call" | custom-call | tf_op jit(solution)/shard_map/newton/pallas_call | solution.py:555
  42.9 0.0 copy-start
  42.9 26.5 %last.1 = (f32[64,768]{1,0:T(8,128)}, f32[64,1024]{1,0:T(8,128)}) custom-call(s32[768,1024]{1,0:T(8,128)} %counts_ref.3, f32[768,1024]{1,0:T(8,128)} %get-tuple-element.8.lin_ref, s32[1,1]{1,0:T(1,128)} %bitcast.12.live_ref, s32[1,1024]{1,0:T(1,128)} %bitcast.24, f32[1,1024]{1,0:T(1,128)} %bitcast.26, f32[16,1024]{1,0:T(8,128)} %cov_ref.3, ...), custom_call_target="tpu_custom_call" | custom-call | tf_op jit(solution)/shard_map/last/pallas_call | solution.py:574
  69.4 0.0 copy-done
  69.4 0.8 %copy.13 = f32[768,32]{0,1:T(8,128)} copy(f32[768,32]{1,0:T(8,128)S(1)} %bitcast.13) | data formatting | bytes 196608
  70.2 1.7 %copy.17 = f32[1024,64]{0,1:T(8,128)} copy(f32[1024,64]{0,1:T(8,128)} %bitcast.18) | data formatting | bytes 524288
  71.9 1.6 %copy.18 = f32[768,64]{0,1:T(8,128)} copy(f32[768,64]{0,1:T(8,128)} %bitcast.20) | data formatting | bytes 393216
Async XLA Ops:
  42.9 26.5 %copy-start = (f32[8,96,32]{2,1,0:T(8,128)S(1)}, f32[8,96,32]{2,1,0:T(8,128)}, u32[]{:S(2)}) copy-start(f32[8,96,32]{2,1,0:T(8,128)} %newton.1.beta_ref) | copy-start | bytes 294916
where the time goes:
time: 73.8 us; the launch traced here: 73.5 us
  Pallas kernels  65.4 us (89%)
  local copies, waits for them, and re-layouts  4.07 us (6%)
  other arithmetic  2.7 us (4%)
  between operations  1.32 us (2%)
    pallas_call x1, Pallas kernels, local_fused(): pl.pallas_call(functools.partial(last_kernel, n, m), out_shape=(shape((la...  26.5 us
    pallas_call x1, Pallas kernels, local_fused(): pl.pallas_call(functools.partial(newton_kernel, n), out_shape=shape((n, r...  21.4 us
    pallas_call x1, Pallas kernels, local_fused(): pl.pallas_call(first_kernel, grid=(steps,), out_shape=(shape((n, rows, wi...  8.87 us
    pallas_call x1, Pallas kernels, local_fused(): pl.pallas_call(functools.partial(totals_kernel, m), out_shape=shape((1, s...  8.6 us
    unnamed x5, local copies, waits for them, and re-layouts  4.07 us
    reduce_sum x1, other arithmetic, local_fused(): part = jnp.sum(counts, axis=0, keepdims=True).astype(F32)  2.11 us

commit v1 on v0

v1 whole, which is shorter than its diff:
```python
import functools

import jax
import jax.numpy as jnp
from jax import lax
from jax.experimental import pallas as pl
from jax.experimental.pallas import tpu as pltpu
from jax.sharding import PartitionSpec as P

GENES = 3072
SPL = 16
BATCHES = 64


ridge_weight = 1.0


def design_rows(knot_bin, depth_frac, cell_covariates):
    levels = jnp.arange(SPL, dtype=jnp.int32)[:, None]
    fraction = depth_frac[None, :]
    hat_basis = jnp.where(levels == knot_bin[None, :], 1.0 - fraction, 0.0)
    hat_basis = hat_basis + jnp.where(levels == knot_bin[None, :] + 1, fraction, 0.0)
    return jnp.concatenate([hat_basis, cell_covariates], axis=0)


def newton_solve(gram_flat, score):
    columns = score.shape[-1]
    identity = jnp.eye(columns, dtype=gram_flat.dtype)
    system = gram_flat.reshape(-1, columns, columns) + ridge_weight * identity
    factor_lower = jnp.linalg.cholesky(system)
    middle = jax.scipy.linalg.solve_triangular(factor_lower, score[..., None], lower=True)
    return jax.scipy.linalg.solve_triangular(factor_lower, middle, lower=True, trans=1)[..., 0]


def local_plain(
    counts,
    batch_id,
    live_cells,
    knot_bin,
    depth_frac,
    cell_covariates,
    coefficients,
    batch_effect,
    factors,
    loadings,
):
    highest = lax.Precision.HIGHEST
    contract = (((1,), (1,)), ((), ()))
    observed = counts.astype(jnp.float32)
    totals = lax.psum(jnp.sum(observed, axis=0), "gene")
    offset = jnp.log((1.0 + totals) / GENES)
    slot_count = observed.shape[1]
    live_mask = (jnp.arange(slot_count, dtype=jnp.int32) < live_cells[0]).astype(jnp.float32)
    design = design_rows(knot_bin, depth_frac, cell_covariates)
    columns = design.shape[0]
    onehot = (jnp.arange(BATCHES, dtype=jnp.int32)[:, None] == batch_id[None, :]).astype(
        jnp.float32
    )
    stacked = jnp.concatenate([design, onehot], axis=0)
    linear = jnp.dot(
        jnp.concatenate([coefficients, batch_effect], axis=1), stacked, precision=highest
    )
    latent = lax.dot_general(loadings, factors, contract, preferred_element_type=jnp.float32)
    linear_pred = offset[None, :] + linear + latent
    expected = jnp.exp(linear_pred)
    weight = expected * live_mask
    residual = (observed - expected) * live_mask
    pairs = (design[:, None, :] * design[None, :, :]).reshape(columns * columns, slot_count)
    gram_part = lax.dot_general(weight, pairs, contract, precision=highest)
    score_part = lax.dot_general(residual, design, contract, precision=highest)
    gram_share, score_share = (
        lax.psum_scatter(gram_part, "cell", scatter_dimension=0, tiled=True),
        lax.psum_scatter(score_part, "cell", scatter_dimension=0, tiled=True),
    )
    step_share = newton_solve(gram_share, score_share)
    beta_step = lax.all_gather(step_share, "cell", axis=0, tiled=True)
    expected_next = jnp.exp(linear_pred + jnp.dot(beta_step, design, precision=highest))
    weight_next = expected_next * live_mask
    residual_next = (observed - expected_next) * live_mask
    factors_wide = factors.astype(jnp.float32)
    loads_wide = loadings.astype(jnp.float32)
    grad_load = jnp.dot(residual_next, factors_wide, precision=highest)
    curv_load = jnp.dot(weight_next, factors_wide * factors_wide, precision=highest)
    back = (((0,), (0,)), ((), ()))
    grad_fact = lax.dot_general(residual_next, loads_wide, back, precision=highest)
    curv_fact = lax.dot_general(weight_next, loads_wide * loads_wide, back, precision=highest)
    grad_load, curv_load = lax.psum((grad_load, curv_load), "cell")
    grad_fact, curv_fact = lax.psum((grad_fact, curv_fact), "gene")
    factor_step = grad_fact / (curv_fact + 1.0)
    loading_score = grad_load / jnp.sqrt(curv_load + 1.0)
    return (beta_step, factor_step, loading_score)


MESH = pl.DeviceIdType.MESH
F32, BF16 = jnp.float32, jnp.bfloat16
VM = pl.BlockSpec(memory_space=pltpu.VMEM)
ROWS_BY_ROWS = (((1,), (1,)), ((), ()))
ACROSS = (((1,), (0,)), ((), ()))
DOWN = (((0,), (0,)), ((), ()))
LIMIT = 60 * 1024 * 1024


def split(x):
    high = x.astype(BF16)
    return high, (x - high.astype(F32)).astype(BF16)


def mul(a, b, dims):
    return lax.dot_general(a, b, dims, preferred_element_type=F32)


def remote(src, dst, send, recv, where):
    return pltpu.make_async_remote_copy(
        src_ref=src, dst_ref=dst, send_sem=send, recv_sem=recv, device_id=where, device_id_type=MESH
    )


def meet_signal(groups):
    barrier = pltpu.get_barrier_semaphore()
    count = 0
    for axis, n in groups:
        me = lax.axis_index(axis)
        for d in range(1, n):
            pl.semaphore_signal(
                barrier, inc=1, device_id={axis: lax.rem(me + d, n)}, device_id_type=MESH
            )
        count += n - 1
    return lambda: pl.semaphore_wait(barrier, count)


def design_of(knot_ref, frac_ref, cov_ref):
    slots = knot_ref.shape[1]
    levels = lax.broadcasted_iota(jnp.int32, (SPL, slots), 0)
    knot, frac = knot_ref[...], frac_ref[...]
    hats = jnp.where(levels == knot, 1.0 - frac, 0.0)
    hats = hats + jnp.where(levels == knot + 1, frac, 0.0)
    return hats, cov_ref[...]


def build_pairs(hats, cov, pair_hi, pair_lo):
    slots = hats.shape[1]
    ncov = cov.shape[0]
    half = ncov // 2

    def put(at, block):
        high, low = split(block)
        pair_hi[at : at + block.shape[0]] = high
        pair_lo[at : at + block.shape[0]] = low

    at = 0
    for p in range(SPL):
        put(at, hats[p : p + 1] * cov)
        at += ncov
    for i in range(half):
        put(at, cov[i : i + 1] * cov)
        at += ncov
    for i in range(half, ncov, 2):
        put(
            at,
            jnp.concatenate(
                [cov[i : i + 1] * cov[half:], cov[i + 1 : i + 2] * cov[half:]], axis=0
            ),
        )
        at += ncov
    put(at, hats * hats)
    at += SPL
    later = jnp.concatenate([hats[1:], jnp.zeros((1, slots), F32)], axis=0)
    put(at, hats * later)
    at += SPL
    put(at, jnp.zeros((SPL + ncov, slots), F32))


def solve(g, x):
    half = SPL // 2
    cov_at, low_at, hat_at = SPL * SPL, SPL * SPL + half * SPL, SPL * SPL + half * SPL + half * half
    off_at, score_at = hat_at + SPL, hat_at + 2 * SPL
    spot = lax.broadcasted_iota(jnp.int32, (half, g.shape[1]), 0)

    def one(block, i):
        return block[i : i + 1]

    lo = {}
    hi = {}
    for i in range(SPL):
        unit = jnp.where(spot == i % half, ridge_weight, 0.0)
        if i < half:
            lo[i] = g[cov_at + i * SPL : cov_at + i * SPL + half] + unit
            hi[i] = g[cov_at + i * SPL + half : cov_at + (i + 1) * SPL]
        else:
            hi[i] = g[low_at + (i - half) * half : low_at + (i - half + 1) * half] + unit
    b_lo = g[score_at + SPL : score_at + SPL + half]
    b_hi = g[score_at + SPL + half : score_at + 2 * SPL]
    sums_lo, sums_hi = g[0:half], g[half:SPL]
    for p in range(1, SPL):
        sums_lo = sums_lo + g[p * SPL : p * SPL + half]
        sums_hi = sums_hi + g[p * SPL + half : (p + 1) * SPL]
    b_lo, b_hi = b_lo - sums_lo, b_hi - sums_hi
    pivot_inv, edge, side_lo, side_hi, rest = [], [], [], [], []
    for p in range(SPL):
        own = g[hat_at + p : hat_at + p + 1]
        after = g[off_at + p : off_at + p + 1]
        d = own + ridge_weight
        u_lo = g[p * SPL : p * SPL + half]
        u_hi = g[p * SPL + half : (p + 1) * SPL]
        b = g[score_at + p : score_at + p + 1] - own - after
        if p > 0:
            b = b - edge[-1]
            ratio = edge[-1] * pivot_inv[-1]
            d = d - ratio * edge[-1]
            u_lo = u_lo - ratio * side_lo[-1]
            u_hi = u_hi - ratio * side_hi[-1]
            b = b - ratio * rest[-1]
        inv = 1.0 / d
        pivot_inv.append(inv)
        edge.append(after)
        side_lo.append(u_lo)
        side_hi.append(u_hi)
        rest.append(b)
        scaled_lo, scaled_hi = u_lo * inv, u_hi * inv
        b_lo = b_lo - scaled_lo * b
        b_hi = b_hi - scaled_hi * b
        for i in range(SPL):
            if i < half:
                f = one(scaled_lo, i)
                lo[i] = lo[i] - f * u_lo
            else:
                f = one(scaled_hi, i - half)
            hi[i] = hi[i] - f * u_hi
    c_inv, c_rest = [], []
    for j in range(SPL):
        if j < half:
            inv = 1.0 / one(lo[j], j)
            b = one(b_lo, j)
            s_lo = lo[j] * inv
            b_lo = b_lo - s_lo * b
        else:
            inv = 1.0 / one(hi[j], j - half)
            b = one(b_hi, j - half)
        s_hi = hi[j] * inv
        b_hi = b_hi - s_hi * b
        c_inv.append(inv)
        c_rest.append(b)
        for i in range(j + 1, SPL):
            if i < half:
                f = one(s_lo, i)
                lo[i] = lo[i] - f * lo[j]
            else:
                f = one(s_hi, i - half)
            hi[i] = hi[i] - f * hi[j]
    for j in reversed(range(SPL)):
        found = c_rest[j] * c_inv[j]
        x[SPL + j : SPL + j + 1] = found
        for i in range(j):
            c_rest[i] = c_rest[i] - (one(hi[i], j - half) if j >= half else one(lo[i], j)) * found
    x_lo, x_hi = x[SPL : SPL + half], x[SPL + half : 2 * SPL]
    after = None
    for p in reversed(range(SPL)):
        gone = jnp.sum(side_lo[p] * x_lo + side_hi[p] * x_hi, axis=0, keepdims=True)
        b = rest[p] - gone
        if after is not None:
            b = b - edge[p] * after
        after = b * pivot_inv[p]
        x[p : p + 1] = after


def all_kernel(
    n, m, counts_hbm, batch_ref, live_ref, knot_ref, frac_ref, cov_ref, coef_ref, shift_ref,
    factors_ref, loads_ref, beta_ref, fs_ref, ls_ref,
    counts, lin, rhs, pair_hi, pair_lo, tally, f_all, l_all, extra, tot_out, tot_in, known_c, known_f,
    w_hi, w_lo, lhs_ref, g, g_pair, g_out, g_far, tall, turned, mine, theirs,
    gl, l_pair, l_out, l_far, my_l, their_l, gf, from_g, my_f, their_f,
    c_sem, t_send, t_recv, gp_send, gp_recv, gf_send, gf_recv, b_send, b_recv,
    lp_send, lp_recv, lf_send, lf_recv, ol_send, ol_recv, z_send, z_recv, of_send, of_recv,
):
    cell, gene = lax.axis_index("cell"), lax.axis_index("gene")
    core, chip = lax.rem(cell, 2), cell // 2
    chips = n // 2
    genes, slots = counts.shape
    block = genes // chips
    rows = genes // n
    latent = loads_ref.shape[0]
    span = slots // m
    arrive = meet_signal((("cell", n), ("gene", m)))
    loads_in = []
    for i in range(n):
        at = pl.ds(i * rows, rows)
        loads_in.append(pltpu.make_async_copy(counts_hbm.at[at], counts.at[at], c_sem.at[i]))
        loads_in[-1].start()
    part = None
    for i in range(n):
        loads_in[i].wait()
        piece = jnp.sum(counts[i * rows : (i + 1) * rows].reshape(rows // 8, 8, slots), axis=0)
        part = piece if part is None else part + piece
    tot_out[...] = jnp.sum(part, axis=0, keepdims=True).astype(F32)
    arrive()
    tot = []
    for d in range(1, m):
        tot.append(
            remote(
                tot_out, tot_in.at[d - 1], t_send.at[d - 1], t_recv.at[d - 1],
                {"gene": lax.rem(gene + d, m)},
            )
        )
        tot[-1].start()

    hats, cov = design_of(knot_ref, frac_ref, cov_ref)
    width = hats.shape[0] + cov.shape[0]
    design_hi, design_lo = split(jnp.concatenate([hats, cov], axis=0))
    hot = lax.broadcasted_iota(jnp.int32, (BATCHES, slots), 0) == batch_ref[...]
    hot = jnp.where(hot, 1.0, 0.0).astype(BF16)
    rhs[0:width] = design_hi
    rhs[width : 2 * width] = design_hi
    rhs[2 * width : 3 * width] = design_lo
    rhs[3 * width : 3 * width + BATCHES] = hot
    rhs[3 * width + BATCHES : 3 * width + 2 * BATCHES] = hot
    rhs[3 * width + 2 * BATCHES :] = factors_ref[...]
    coef_hi, coef_lo = split(coef_ref[...])
    shift_hi, shift_lo = split(shift_ref[...])
    lhs = jnp.concatenate([coef_hi, coef_lo, coef_hi, shift_hi, shift_lo, loads_ref[...]], axis=0)
    lin[...] = mul(lhs, rhs[...], DOWN)
    build_pairs(hats, cov, pair_hi, pair_lo)
    live = lax.broadcasted_iota(jnp.int32, (1, slots), 1) < live_ref[...]
    mask = jnp.where(live, 1.0, 0.0)
    mask_bf = mask.astype(BF16)
    tally[0:width] = design_hi * mask_bf
    tally[width : 2 * width] = design_lo * mask_bf
    factors_live = factors_ref[...].astype(F32) * mask
    tally[2 * width :] = factors_live.astype(BF16)
    f_hi, f_lo = split(factors_live * factors_live)
    f_all[0:latent] = factors_live.astype(BF16)
    f_all[latent : 2 * latent] = f_hi
    f_all[2 * latent :] = f_lo
    loads_wide = loads_ref[...].astype(F32)
    l_hi, l_lo = split(loads_wide * loads_wide)
    l_all[0:latent] = loads_ref[...]
    l_all[latent : 2 * latent] = l_hi
    l_all[2 * latent :] = l_lo
    counts_bf = counts[...].astype(F32).astype(BF16)
    known_c[...] = mul(counts_bf, tally[...], ROWS_BY_ROWS)
    known_f[...] = mul(l_all[0:latent], counts_bf, ACROSS) * mask

    total = tot_out[...]
    for d in range(1, m):
        tot[d - 1].wait()
        total = total + tot_in[d - 1]
    extra[0:1] = jnp.where(live, jnp.log((1.0 + total) / GENES), -1e30)

    places = [chips - 1 - chip, chip + 1 - 2 * lax.rem(chip, 2), lax.rem(chip + 2, chips), chip]

    def hand_on(j, mine_ref, pair_ref, copy, out_ref, far_ref, send, recv):
        copy.wait()
        if j == chips - 1:
            return None
        out_ref[j] = mine_ref[j, core] + pair_ref[j]
        far = remote(
            out_ref.at[j], far_ref.at[j], send.at[j], recv.at[j], {"cell": 2 * places[j] + core}
        )
        far.start()
        return far

    partner = cell + 1 - 2 * core
    wide = g.shape[3]
    pair, far = [], []
    for j in range(chips):
        at = pl.ds(pl.multiple_of(places[j] * block, block), block)
        linear = lin[at] + extra[0:1]
        lin[at] = linear
        high, low = split(jnp.exp(linear))
        both = mul(jnp.concatenate([high, low], axis=0), pair_hi[...], ROWS_BY_ROWS)
        gram = both[:block] + both[block:] + mul(high, pair_lo[...], ROWS_BY_ROWS)
        counted = known_c[at, 0:width] + known_c[at, width : 2 * width]
        g[j, :, :, : wide - width] = gram[:, : wide - width].reshape(2, rows, wide - width)
        g[j, :, :, wide - width :] = counted.reshape(2, rows, width)
        pair.append(
            remote(g.at[j, 1 - core], g_pair.at[j], gp_send.at[j], gp_recv.at[j], {"cell": partner})
        )
        pair[-1].start()
        if j > 0:
            far.append(
                hand_on(j - 1, g, g_pair, pair[j - 1], g_out, g_far, gf_send, gf_recv)
            )
    hand_on(chips - 1, g, g_pair, pair[-1], g_out, g_far, gf_send, gf_recv)
    total = g[chips - 1, core] + g_pair[chips - 1]
    for j in range(chips - 1):
        far[j].wait()
        total = total + g_far[j]
    tall[0:rows] = total
    if rows < 128:
        tall[rows:128] = jnp.zeros((128 - rows, wide), F32)
    turned[...] = tall[...].T
    solve(turned, mine)
    out = []
    for d in range(1, n):
        out.append(
            remote(
                mine, theirs.at[cell], b_send.at[d - 1], b_recv.at[d - 1],
                {"cell": lax.rem(cell + d, n)},
            )
        )
        out[-1].start()
    theirs[cell] = mine[...]
    for d in range(1, n):
        out[d - 1].wait()
    for o in range(n):
        beta_ref[:, o * rows : (o + 1) * rows] = theirs[o, :, :rows]
    beta_hi, beta_lo = split(beta_ref[...])
    lhs_ref[...] = jnp.concatenate([beta_hi, beta_lo, beta_hi], axis=0).astype(F32).T.astype(BF16)

    along = []
    for d in list(range(1, m)) + [0]:
        to = lax.rem(gene + d, m)
        cols = pl.ds(pl.multiple_of(to * span, span), span)
        delta = mul(lhs_ref[...], rhs[0 : 3 * width, cols], ACROSS)
        high, low = split(jnp.exp(lin[:, cols] + delta))
        w_hi[:, cols] = high
        w_lo[:, cols] = low
        first = mul(l_all[...], high, ACROSS)
        second = mul(l_all[0 : 2 * latent], low, ACROSS)
        gf[d, :latent] = known_f[:, cols] - first[:latent] - second[:latent]
        gf[d, latent:] = first[latent : 2 * latent] + first[2 * latent :] + second[latent:]
        if d > 0:
            along.append(
                remote(gf.at[d], from_g.at[d - 1], z_send.at[d - 1], z_recv.at[d - 1], {"gene": to})
            )
            along[-1].start()
    lpair, lfar = [], []
    for j in range(chips):
        at = pl.ds(pl.multiple_of(places[j] * block, block), block)
        first = mul(w_hi[at], f_all[...], ROWS_BY_ROWS)
        second = mul(w_lo[at], f_all[0 : 2 * latent], ROWS_BY_ROWS)
        grad = known_c[at, 2 * width :] - first[:, :latent] - second[:, :latent]
        curv = first[:, latent : 2 * latent] + first[:, 2 * latent :] + second[:, latent:]
        gl[j] = jnp.concatenate([grad, curv], axis=1).reshape(2, rows, 2 * latent)
        lpair.append(
            remote(gl.at[j, 1 - core], l_pair.at[j], lp_send.at[j], lp_recv.at[j], {"cell": partner})
        )
        lpair[-1].start()
        if j > 0:
            lfar.append(
                hand_on(j - 1, gl, l_pair, lpair[j - 1], l_out, l_far, lf_send, lf_recv)
            )
    hand_on(chips - 1, gl, l_pair, lpair[-1], l_out, l_far, lf_send, lf_recv)
    total = gl[chips - 1, core] + l_pair[chips - 1]
    for j in range(chips - 1):
        lfar[j].wait()
        total = total + l_far[j]
    if rows < 128:
        total = jnp.concatenate([total, jnp.zeros((128 - rows, 2 * latent), F32)], axis=0)
    total = total.T
    my_l[...] = total[:latent] / jnp.sqrt(total[latent:] + 1.0)
    out_l, out_f = [], []
    for d in range(1, n):
        out_l.append(
            remote(
                my_l, their_l.at[cell], ol_send.at[d - 1], ol_recv.at[d - 1],
                {"cell": lax.rem(cell + d, n)},
            )
        )
        out_l[-1].start()
    their_l[cell] = my_l[...]
    total = gf[0]
    for d in range(1, m):
        along[d - 1].wait()
        total = total + from_g[d - 1]
    my_f[...] = total[:latent] / (total[latent:] + 1.0)
    for d in range(1, m):
        out_f.append(
            remote(
                my_f, their_f.at[gene], of_send.at[d - 1], of_recv.at[d - 1],
                {"gene": lax.rem(gene + d, m)},
            )
        )
        out_f[-1].start()
    their_f[gene] = my_f[...]
    for d in range(1, n):
        out_l[d - 1].wait()
    for o in range(n):
        ls_ref[:, o * rows : (o + 1) * rows] = their_l[o, :, :rows]
    for d in range(1, m):
        out_f[d - 1].wait()
    for o in range(m):
        fs_ref[:, o * span : (o + 1) * span] = their_f[o]


def pass_on(*refs):
    count = len(refs) // 2
    for source, target in zip(refs[:count], refs[count:]):
        target[...] = source[...]


def local_fused(
    n, m, counts, batch_id, live_cells, knot_bin, depth_frac, cell_covariates, coefficients,
    batch_effect, factors, loadings,
):
    genes, slots = counts.shape
    rows, span, latent = genes // n, slots // m, factors.shape[1]
    ncov = cell_covariates.shape[0]
    width = SPL + ncov
    wide = SPL * ncov + ncov * ncov * 3 // 4 + 2 * SPL + width
    chips = n // 2
    dma = pltpu.SemaphoreType.DMA
    shape = jax.ShapeDtypeStruct
    vmem = pltpu.VMEM

    def params(**kw):
        return pltpu.CompilerParams(vmem_limit_bytes=LIMIT, **kw)

    knot, frac, batch = (v.reshape(1, slots) for v in (knot_bin, depth_frac, batch_id))
    shapes = (shape((width, genes), F32), shape((latent, slots), F32), shape((latent, genes), F32))
    found = pl.pallas_call(
        functools.partial(all_kernel, n, m),
        out_shape=shapes,
        in_specs=[pl.BlockSpec(memory_space=pl.ANY)] + [VM] * 9,
        out_specs=(VM, VM, VM),
        scratch_shapes=[
            vmem((genes, slots), jnp.int32),
            vmem((genes, slots), F32),
            vmem((3 * width + 2 * BATCHES + latent, slots), BF16),
            vmem((wide, slots), BF16),
            vmem((wide, slots), BF16),
            vmem((2 * width + latent, slots), BF16),
            vmem((3 * latent, slots), BF16),
            vmem((3 * latent, genes), BF16),
            vmem((8, slots), F32),
            vmem((1, slots), F32),
            vmem((m - 1, 1, slots), F32),
            vmem((genes, 2 * width + latent), F32),
            vmem((latent, slots), F32),
            vmem((genes, slots), BF16),
            vmem((genes, slots), BF16),
            vmem((genes, 3 * width), BF16),
            vmem((chips, 2, rows, wide), F32),
            vmem((chips, rows, wide), F32),
            vmem((chips - 1, rows, wide), F32),
            vmem((chips - 1, rows, wide), F32),
            vmem((128, wide), F32),
            vmem((wide, 128), F32),
            vmem((width, 128), F32),
            vmem((n, width, 128), F32),
            vmem((chips, 2, rows, 2 * latent), F32),
            vmem((chips, rows, 2 * latent), F32),
            vmem((chips - 1, rows, 2 * latent), F32),
            vmem((chips - 1, rows, 2 * latent), F32),
            vmem((latent, 128), F32),
            vmem((n, latent, 128), F32),
            vmem((m, 2 * latent, span), F32),
            vmem((m - 1, 2 * latent, span), F32),
            vmem((latent, span), F32),
            vmem((m, latent, span), F32),
            dma((n,)), dma((m - 1,)), dma((m - 1,)),
            dma((chips,)), dma((chips,)), dma((chips - 1,)), dma((chips - 1,)),
            dma((n - 1,)), dma((n - 1,)),
            dma((chips,)), dma((chips,)), dma((chips - 1,)), dma((chips - 1,)),
            dma((n - 1,)), dma((n - 1,)), dma((m - 1,)), dma((m - 1,)), dma((m - 1,)), dma((m - 1,)),
        ],
        compiler_params=params(collective_id=0, has_side_effects=True),
        name="step",
    )(
        counts, batch, live_cells.reshape(1, 1), knot, frac, cell_covariates, coefficients.T,
        batch_effect.T, factors.T, loadings.T,
    )
    beta, fs, ls = pl.pallas_call(
        pass_on, out_shape=shapes, in_specs=[VM] * 3, out_specs=(VM, VM, VM),
        compiler_params=params(), name="finish",
    )(*found)
    return beta.T, fs.T, ls.T


def local(n, m, *args):
    counts, cov, factors = args[0], args[5], args[8]
    genes, slots = counts.shape
    fits = (
        n == 8
        and m > 1
        and genes % (16 * n) == 0
        and genes // n <= 128
        and slots % (128 * m) == 0
        and cov.shape[0] == SPL
        and factors.shape[1] == 64
    )
    if fits:
        return local_fused(n, m, *args)
    return local_plain(*args)


def solution(mesh):
    placed = (
        P("gene", "cell"),
        P("cell"),
        P("cell"),
        P("cell"),
        P("cell"),
        P(None, "cell"),
        P("gene", None),
        P("gene", None),
        P("cell", None),
        P("gene", None),
    )
    return jax.shard_map(
        functools.partial(local, mesh.shape["cell"], mesh.shape["gene"]),
        mesh=mesh,
        in_specs=placed,
        out_specs=(P("gene", None), P("cell", None), P("gene", None)),
        check_vma=False,
    )
```

time: 73.8 us -> 51.5 us (0.70)
  Pallas kernels: 65.4 us -> 50 us
  local copies, waits for them, and re-layouts: 4.07 us -> 0 us
  other arithmetic: 2.7 us -> 0 us
    pallas_call x4 -> x2, Pallas kernels: 65.4 us -> 50 us  [the longest x1 48.1 us: local_fused(): pl.pallas_call(functools.partial(all_kernel, n, m), out_shape=shapes, in_...]
    unnamed x5 -> x0, local copies, waits for them, and re-layouts: 4.07 us -> none
    reduce_sum x1 -> x0, other arithmetic: 2.11 us -> none  [local_fused(): part = jnp.sum(counts, axis=0, keepdims=True).astype(F32)]
where the time goes in v1:
time: 51.5 us; the launch traced here: 51.3 us
  Pallas kernels  50 us (97%)
  between operations  1.29 us (3%)
    pallas_call x1, Pallas kernels, local_fused(): pl.pallas_call(functools.partial(all_kernel, n, m), out_shape=shapes, in_...  48.1 us
    pallas_call x1, Pallas kernels, local_fused(): pl.pallas_call(pass_on, out_shape=shapes, in_specs=[VM] * 3, out_specs=(V...  1.87 us

profile of v1, /device:TPU:0, one launch (start us, length us, event | category | flops | bytes accessed | tf_op | source)
XLA Modules:
  0.0 51.3 jit_solution(16532041403886163975)
XLA Ops:
  1.3 48.1 %step.1 = (f32[32,768]{1,0:T(8,128)}, f32[64,1024]{1,0:T(8,128)}, f32[64,768]{1,0:T(8,128)}) custom-call(s32[768,1024]{1,0:T(8,128)} %counts_hbm.1, s32[1,1024]{1,0:T(1,128)} %bitcast.16, s32[1,1]{1,0:T(1,128)} %bitcast.11.live_ref, s32[1,1024]{1,0:T(1,128)} %bitcast.17, f32[1,1024]{1,0:T(1,128)} %bitcast.18, f32[16,1024]{1,0:T(8,128)} %cov_ref.1, ...), custom_call_target="tpu_custom_call" | custom-call | tf_op jit(solution)/shard_map/step/pallas_call | solution.py:510
  49.4 1.9 %finish.1 = (f32[32,768]{1,0:T(8,128)}, f32[64,1024]{1,0:T(8,128)}, f32[64,768]{1,0:T(8,128)}) custom-call(f32[32,768]{1,0:T(8,128)} %get-tuple-element.9.refs_0_, f32[64,1024]{1,0:T(8,128)} %get-tuple-element.10.refs_1_, f32[64,768]{1,0:T(8,128)} %get-tuple-element.11.refs_2_), custom_call_target="tpu_custom_call" | custom-call | tf_op jit(solution)/shard_map/finish/pallas_call | solution.py:562

commit v2 on v1

--- a/solution.py
+++ b/solution.py
@@ -97,7 +97,7 @@
 ROWS_BY_ROWS = (((1,), (1,)), ((), ()))
 ACROSS = (((1,), (0,)), ((), ()))
 DOWN = (((0,), (0,)), ((), ()))
-LIMIT = 60 * 1024 * 1024
+LIMIT = 40 * 1024 * 1024
 
 
 def split(x):
@@ -264,13 +264,15 @@
 
 
 def all_kernel(
-    n, m, counts_hbm, batch_ref, live_ref, knot_ref, frac_ref, cov_ref, coef_ref, shift_ref,
-    factors_ref, loads_ref, beta_ref, fs_ref, ls_ref,
+    n, m, counts_hbm, batch_hbm, live_ref, knot_hbm, frac_hbm, cov_hbm, coef_hbm, shift_hbm,
+    factors_hbm, loads_hbm, beta_ref, fs_ref, ls_ref,
+    batch_ref, knot_ref, frac_ref, cov_ref, coef_ref, shift_ref, factors_ref, loads_ref,
     counts, lin, rhs, pair_hi, pair_lo, tally, f_all, l_all, extra, tot_out, tot_in, known_c, known_f,
-    w_hi, w_lo, lhs_ref, g, g_pair, g_out, g_far, tall, turned, mine, theirs,
-    gl, l_pair, l_out, l_far, my_l, their_l, gf, from_g, my_f, their_f,
-    c_sem, t_send, t_recv, gp_send, gp_recv, gf_send, gf_recv, b_send, b_recv,
-    lp_send, lp_recv, lf_send, lf_recv, ol_send, ol_recv, z_send, z_recv, of_send, of_recv,
+    w_hi, w_lo, lhs_ref, g, g_pair, g_out, g_side, g_far, tall, turned, mine, theirs,
+    gl, l_pair, l_out, l_far, my_l, their_l, gf, z_in, z_relay, z_sum, my_f, their_f,
+    c_sem, i_sem, t_send, t_recv, gp_send, gp_recv, gs_send, gs_recv, gf_send, gf_recv,
+    b_send, b_recv, lp_send, lp_recv, lf_send, lf_recv, ol_send, ol_recv, z_send, z_recv,
+    of_send, of_recv,
 ):
     cell, gene = lax.axis_index("cell"), lax.axis_index("gene")
     core, chip = lax.rem(cell, 2), cell // 2
@@ -286,12 +288,24 @@
         at = pl.ds(i * rows, rows)
         loads_in.append(pltpu.make_async_copy(counts_hbm.at[at], counts.at[at], c_sem.at[i]))
         loads_in[-1].start()
+    small = []
+    for i, (source, target) in enumerate(
+        (
+            (batch_hbm, batch_ref), (knot_hbm, knot_ref), (frac_hbm, frac_ref), (cov_hbm, cov_ref),
+            (coef_hbm, coef_ref), (shift_hbm, shift_ref), (factors_hbm, factors_ref),
+            (loads_hbm, loads_ref),
+        )
+    ):
+        small.append(pltpu.make_async_copy(source, target, i_sem.at[i]))
+        small[-1].start()
     part = None
     for i in range(n):
         loads_in[i].wait()
         piece = jnp.sum(counts[i * rows : (i + 1) * rows].reshape(rows // 8, 8, slots), axis=0)
         part = piece if part is None else part + piece
     tot_out[...] = jnp.sum(part, axis=0, keepdims=True).astype(F32)
+    for copy in small:
+        copy.wait()
     arrive()
     tot = []
     for d in range(1, m):
@@ -319,25 +333,14 @@
     lhs = jnp.concatenate([coef_hi, coef_lo, coef_hi, shift_hi, shift_lo, loads_ref[...]], axis=0)
     lin[...] = mul(lhs, rhs[...], DOWN)
     build_pairs(hats, cov, pair_hi, pair_lo)
-    live = lax.broadcasted_iota(jnp.int32, (1, slots), 1) < live_ref[...]
+    live = lax.broadcasted_iota(jnp.int32, (1, slots), 1) < live_ref[0]
     mask = jnp.where(live, 1.0, 0.0)
     mask_bf = mask.astype(BF16)
+    factors_live = factors_ref[...].astype(F32) * mask
     tally[0:width] = design_hi * mask_bf
     tally[width : 2 * width] = design_lo * mask_bf
-    factors_live = factors_ref[...].astype(F32) * mask
     tally[2 * width :] = factors_live.astype(BF16)
-    f_hi, f_lo = split(factors_live * factors_live)
-    f_all[0:latent] = factors_live.astype(BF16)
-    f_all[latent : 2 * latent] = f_hi
-    f_all[2 * latent :] = f_lo
-    loads_wide = loads_ref[...].astype(F32)
-    l_hi, l_lo = split(loads_wide * loads_wide)
-    l_all[0:latent] = loads_ref[...]
-    l_all[latent : 2 * latent] = l_hi
-    l_all[2 * latent :] = l_lo
-    counts_bf = counts[...].astype(F32).astype(BF16)
-    known_c[...] = mul(counts_bf, tally[...], ROWS_BY_ROWS)
-    known_f[...] = mul(l_all[0:latent], counts_bf, ACROSS) * mask
+    known_c[...] = mul(counts[...].astype(F32).astype(BF16), tally[...], ROWS_BY_ROWS)
 
     total = tot_out[...]
     for d in range(1, m):
@@ -345,23 +348,14 @@
         total = total + tot_in[d - 1]
     extra[0:1] = jnp.where(live, jnp.log((1.0 + total) / GENES), -1e30)
 
-    places = [chips - 1 - chip, chip + 1 - 2 * lax.rem(chip, 2), lax.rem(chip + 2, chips), chip]
-
-    def hand_on(j, mine_ref, pair_ref, copy, out_ref, far_ref, send, recv):
-        copy.wait()
-        if j == chips - 1:
-            return None
-        out_ref[j] = mine_ref[j, core] + pair_ref[j]
-        far = remote(
-            out_ref.at[j], far_ref.at[j], send.at[j], recv.at[j], {"cell": 2 * places[j] + core}
-        )
-        far.start()
-        return far
-
+    beside, above = chip + 1 - 2 * lax.rem(chip, 2), lax.rem(chip + 2, chips)
+    places = [chips - 1 - chip, beside, above, chip]
     partner = cell + 1 - 2 * core
     wide = g.shape[3]
-    pair, far = [], []
-    for j in range(chips):
+    cut = rows // 2
+    upper, lower = slice(0, cut), slice(cut, rows)
+
+    def gram_chunk(j):
         at = pl.ds(pl.multiple_of(places[j] * block, block), block)
         linear = lin[at] + extra[0:1]
         lin[at] = linear
@@ -371,19 +365,55 @@
         counted = known_c[at, 0:width] + known_c[at, width : 2 * width]
         g[j, :, :, : wide - width] = gram[:, : wide - width].reshape(2, rows, wide - width)
         g[j, :, :, wide - width :] = counted.reshape(2, rows, width)
-        pair.append(
-            remote(g.at[j, 1 - core], g_pair.at[j], gp_send.at[j], gp_recv.at[j], {"cell": partner})
+        copy = remote(
+            g.at[j, 1 - core], g_pair.at[j], gp_send.at[j], gp_recv.at[j], {"cell": partner}
         )
-        pair[-1].start()
-        if j > 0:
-            far.append(
-                hand_on(j - 1, g, g_pair, pair[j - 1], g_out, g_far, gf_send, gf_recv)
-            )
-    hand_on(chips - 1, g, g_pair, pair[-1], g_out, g_far, gf_send, gf_recv)
-    total = g[chips - 1, core] + g_pair[chips - 1]
-    for j in range(chips - 1):
-        far[j].wait()
-        total = total + g_far[j]
+        copy.start()
+        return copy
+
+    def onward(j, part, target, send, recv, place):
+        copy = remote(g_out.at[j, part], target, send, recv, {"cell": 2 * place + core})
+        copy.start()
+        return copy
+
+    pair = [gram_chunk(0), gram_chunk(1)]
+    pair[0].wait()
+    g_out[0] = g[0, core] + g_pair[0]
+    side = [
+        onward(0, upper, g_side.at[0], gs_send.at[0], gs_recv.at[0], beside),
+        onward(0, lower, g_side.at[1], gs_send.at[1], gs_recv.at[1], above),
+    ]
+    pair.append(gram_chunk(2))
+    pair[1].wait()
+    g_out[1, upper] = g[1, core, upper] + g_pair[1, upper]
+    far = [onward(1, upper, g_far.at[0, upper], gf_send.at[0], gf_recv.at[0], beside)]
+    pair.append(gram_chunk(3))
+    pair[2].wait()
+    g_out[2, lower] = g[2, core, lower] + g_pair[2, lower]
+    far.append(onward(2, lower, g_far.at[1, lower], gf_send.at[1], gf_recv.at[1], above))
+
+    f_hi, f_lo = split(factors_live * factors_live)
+    f_all[0:latent] = tally[2 * width :]
+    f_all[latent : 2 * latent] = f_hi
+    f_all[2 * latent :] = f_lo
+    loads_wide = loads_ref[...].astype(F32)
+    l_hi, l_lo = split(loads_wide * loads_wide)
+    l_all[0:latent] = loads_ref[...]
+    l_all[latent : 2 * latent] = l_hi
+    l_all[2 * latent :] = l_lo
+
+    side[1].wait()
+    g_out[1, lower] = g[1, core, lower] + g_pair[1, lower] + g_side[1]
+    far.append(onward(1, lower, g_far.at[0, lower], gf_send.at[2], gf_recv.at[2], beside))
+    side[0].wait()
+    g_out[2, upper] = g[2, core, upper] + g_pair[2, upper] + g_side[0]
+    far.append(onward(2, upper, g_far.at[1, upper], gf_send.at[3], gf_recv.at[3], above))
+    known_f[...] = mul(l_all[0:latent], counts[...].astype(F32).astype(BF16), ACROSS) * mask
+    pair[3].wait()
+    total = g[3, core] + g_pair[3]
+    for copy in far:
+        copy.wait()
+    total = total + g_far[0] + g_far[1]
     tall[0:rows] = total
     if rows < 128:
         tall[rows:128] = jnp.zeros((128 - rows, wide), F32)
@@ -406,24 +436,54 @@
     beta_hi, beta_lo = split(beta_ref[...])
     lhs_ref[...] = jnp.concatenate([beta_hi, beta_lo, beta_hi], axis=0).astype(F32).T.astype(BF16)
 
-    along = []
-    for d in list(range(1, m)) + [0]:
-        to = lax.rem(gene + d, m)
-        cols = pl.ds(pl.multiple_of(to * span, span), span)
+    row = gene // 2
+    middle = lax.rem(gene + row, 2)
+    near = gene + 1 - 2 * lax.rem(gene, 2)
+    far_mid, far_end = 2 - row, 3 - 3 * row
+
+    def fact_chunk(j, owner):
+        cols = pl.ds(pl.multiple_of(owner * span, span), span)
         delta = mul(lhs_ref[...], rhs[0 : 3 * width, cols], ACROSS)
         high, low = split(jnp.exp(lin[:, cols] + delta))
         w_hi[:, cols] = high
         w_lo[:, cols] = low
         first = mul(l_all[...], high, ACROSS)
         second = mul(l_all[0 : 2 * latent], low, ACROSS)
-        gf[d, :latent] = known_f[:, cols] - first[:latent] - second[:latent]
-        gf[d, latent:] = first[latent : 2 * latent] + first[2 * latent :] + second[latent:]
-        if d > 0:
-            along.append(
-                remote(gf.at[d], from_g.at[d - 1], z_send.at[d - 1], z_recv.at[d - 1], {"gene": to})
+        gf[j, :latent] = known_f[:, cols] - first[:latent] - second[:latent]
+        gf[j, latent:] = first[latent : 2 * latent] + first[2 * latent :] + second[latent:]
+
+    def along(j, target, k, slot, place):
+        return remote(gf.at[j], target, z_send.at[k], z_recv.at[slot], {"gene": place})
+
+    relay = along(0, z_relay, 0, 3, near)
+    joined = along(0, z_in.at[1], 0, 1, far_mid)
+    straight = along(1, z_in.at[2 - middle], 1, 2 - middle, far_end)
+    close = along(2, z_in.at[0], 2, 0, near)
+    fact_chunk(0, far_mid)
+
+    @pl.when(middle == 0)
+    def _():
+        relay.start()
+
+    fact_chunk(1, far_end)
+    straight.start()
+    fact_chunk(2, near)
+    close.start()
+    fact_chunk(3, gene)
+
+    lpair, lfar = [], []
+
+    def hand_on(j):
+        lpair[j].wait()
+        l_out[j] = gl[j, core] + l_pair[j]
+        lfar.append(
+            remote(
+                l_out.at[j], l_far.at[j], lf_send.at[j], lf_recv.at[j],
+                {"cell": 2 * places[j] + core},
             )
-            along[-1].start()
-    lpair, lfar = [], []
+        )
+        lfar[-1].start()
+
     for j in range(chips):
         at = pl.ds(pl.multiple_of(places[j] * block, block), block)
         first = mul(w_hi[at], f_all[...], ROWS_BY_ROWS)
@@ -436,10 +496,15 @@
         )
         lpair[-1].start()
         if j > 0:
-            lfar.append(
-                hand_on(j - 1, gl, l_pair, lpair[j - 1], l_out, l_far, lf_send, lf_recv)
-            )
-    hand_on(chips - 1, gl, l_pair, lpair[-1], l_out, l_far, lf_send, lf_recv)
+            hand_on(j - 1)
+
+    @pl.when(middle == 1)
+    def _():
+        relay.wait_recv()
+        gf[0] = gf[0] + z_relay[...]
+        joined.start()
+
+    lpair[-1].wait()
     total = gl[chips - 1, core] + l_pair[chips - 1]
     for j in range(chips - 1):
         lfar[j].wait()
@@ -448,7 +513,7 @@
         total = jnp.concatenate([total, jnp.zeros((128 - rows, 2 * latent), F32)], axis=0)
     total = total.T
     my_l[...] = total[:latent] / jnp.sqrt(total[latent:] + 1.0)
-    out_l, out_f = [], []
+    out_l = []
     for d in range(1, n):
         out_l.append(
             remote(
@@ -458,26 +523,61 @@
         )
         out_l[-1].start()
     their_l[cell] = my_l[...]
-    total = gf[0]
-    for d in range(1, m):
-        along[d - 1].wait()
-        total = total + from_g[d - 1]
+
+    close.wait()
+    z_sum[...] = gf[3] + z_in[0]
+
+    @pl.when(middle == 0)
+    def _():
+        straight.wait()
+        z_sum[...] += z_in[2]
+        joined.wait_recv()
+        relay.wait_send()
+
+    @pl.when(middle == 1)
+    def _():
+        straight.wait_send()
+        joined.wait()
+
+    total = z_sum[...] + z_in[1]
     my_f[...] = total[:latent] / (total[latent:] + 1.0)
-    for d in range(1, m):
-        out_f.append(
-            remote(
-                my_f, their_f.at[gene], of_send.at[d - 1], of_recv.at[d - 1],
-                {"gene": lax.rem(gene + d, m)},
-            )
-        )
-        out_f[-1].start()
+
+    def give(source, owner, k, place):
+        return remote(source, their_f.at[owner], of_send.at[k], of_recv.at[owner], {"gene": place})
+
+    give_a = give(my_f, gene, 0, far_end + middle * (far_mid - far_end))
+    give_b = give(my_f, gene, 1, far_mid + middle * (near - far_mid))
+    give_c = give(my_f, gene, 2, near)
+    pass_c = give(their_f.at[far_mid], far_mid, 2, near)
+    give_a.start()
+    give_b.start()
+
+    @pl.when(middle == 0)
+    def _():
+        give_c.start()
+
     their_f[gene] = my_f[...]
+
+    @pl.when(middle == 1)
+    def _():
+        pass_c.wait_recv()
+        pass_c.start()
+
     for d in range(1, n):
         out_l[d - 1].wait()
     for o in range(n):
         ls_ref[:, o * rows : (o + 1) * rows] = their_l[o, :, :rows]
-    for d in range(1, m):
-        out_f[d - 1].wait()
+
+    give(my_f, near, 0, near).wait_recv()
+    give(my_f, far_end, 0, near).wait_recv()
+
+    @pl.when(middle == 0)
+    def _():
+        pass_c.wait_recv()
+
+    give_a.wait_send()
+    give_b.wait_send()
+    give_c.wait_send()
     for o in range(m):
         fs_ref[:, o * span : (o + 1) * span] = their_f[o]
 
@@ -505,14 +605,26 @@
     def params(**kw):
         return pltpu.CompilerParams(vmem_limit_bytes=LIMIT, **kw)
 
+    def stay(x):
+        return pltpu.with_memory_space_constraint(x, pltpu.HBM)
+
     knot, frac, batch = (v.reshape(1, slots) for v in (knot_bin, depth_frac, batch_id))
     shapes = (shape((width, genes), F32), shape((latent, slots), F32), shape((latent, genes), F32))
+    there = pl.BlockSpec(memory_space=pl.ANY)
     found = pl.pallas_call(
         functools.partial(all_kernel, n, m),
         out_shape=shapes,
-        in_specs=[pl.BlockSpec(memory_space=pl.ANY)] + [VM] * 9,
+        in_specs=[there, there, pl.BlockSpec(memory_space=pltpu.SMEM)] + [there] * 7,
         out_specs=(VM, VM, VM),
         scratch_shapes=[
+            vmem((1, slots), jnp.int32),
+            vmem((1, slots), jnp.int32),
+            vmem((1, slots), F32),
+            vmem((ncov, slots), F32),
+            vmem((width, genes), F32),
+            vmem((BATCHES, genes), F32),
+            vmem((latent, slots), BF16),
+            vmem((latent, genes), BF16),
             vmem((genes, slots), jnp.int32),
             vmem((genes, slots), F32),
             vmem((3 * width + 2 * BATCHES + latent, slots), BF16),
@@ -532,7 +644,8 @@
             vmem((chips, 2, rows, wide), F32),
             vmem((chips, rows, wide), F32),
             vmem((chips - 1, rows, wide), F32),
-            vmem((chips - 1, rows, wide), F32),
+            vmem((2, rows // 2, wide), F32),
+            vmem((2, rows, wide), F32),
             vmem((128, wide), F32),
             vmem((wide, 128), F32),
             vmem((width, 128), F32),
@@ -545,19 +658,21 @@
             vmem((n, latent, 128), F32),
             vmem((m, 2 * latent, span), F32),
             vmem((m - 1, 2 * latent, span), F32),
+            vmem((2 * latent, span), F32),
+            vmem((2 * latent, span), F32),
             vmem((latent, span), F32),
             vmem((m, latent, span), F32),
-            dma((n,)), dma((m - 1,)), dma((m - 1,)),
-            dma((chips,)), dma((chips,)), dma((chips - 1,)), dma((chips - 1,)),
+            dma((n,)), dma((8,)), dma((m - 1,)), dma((m - 1,)),
+            dma((chips,)), dma((chips,)), dma((2,)), dma((2,)), dma((4,)), dma((4,)),
             dma((n - 1,)), dma((n - 1,)),
             dma((chips,)), dma((chips,)), dma((chips - 1,)), dma((chips - 1,)),
-            dma((n - 1,)), dma((n - 1,)), dma((m - 1,)), dma((m - 1,)), dma((m - 1,)), dma((m - 1,)),
+            dma((n - 1,)), dma((n - 1,)), dma((m - 1,)), dma((m,)), dma((m - 1,)), dma((m,)),
         ],
         compiler_params=params(collective_id=0, has_side_effects=True),
         name="step",
     )(
-        counts, batch, live_cells.reshape(1, 1), knot, frac, cell_covariates, coefficients.T,
-        batch_effect.T, factors.T, loadings.T,
+        stay(counts), stay(batch), live_cells, stay(knot), stay(frac), stay(cell_covariates),
+        stay(coefficients.T), stay(batch_effect.T), stay(factors.T), stay(loadings.T),
     )
     beta, fs, ls = pl.pallas_call(
         pass_on, out_shape=shapes, in_specs=[VM] * 3, out_specs=(VM, VM, VM),
@@ -571,7 +686,7 @@
     genes, slots = counts.shape
     fits = (
         n == 8
-        and m > 1
+        and m == 4
         and genes % (16 * n) == 0
         and genes // n <= 128
         and slots % (128 * m) == 0

time: 51.5 us -> 49.9 us (0.969)
  Pallas kernels: 50 us -> 48.5 us
    pallas_call x1, Pallas kernels: 1.87 us -> 0.83 us  [local_fused(): pl.pallas_call(pass_on, out_shape=shapes, in_specs=[VM] * 3, out_specs=(V...]
where the time goes in v2:
time: 49.9 us; the launch traced here: 49.8 us
  Pallas kernels  48.5 us (97%)
  between operations  1.29 us (3%)
    pallas_call x1, Pallas kernels, local_fused(): pl.pallas_call(functools.partial(all_kernel, n, m), out_shape=shapes, in_...  47.6 us

profile of v2, /device:TPU:0, one launch (start us, length us, event | category | flops | bytes accessed | tf_op | source)
XLA Modules:
  0.0 49.8 jit_solution(6969288678329473105)
XLA Ops:
  1.3 47.6 %step.1 = (f32[32,768]{1,0:T(8,128)S(1)}, f32[64,1024]{1,0:T(8,128)S(1)}, f32[64,768]{1,0:T(8,128)S(1)}) custom-call(s32[768,1024]{1,0:T(8,128)} %counts_hbm.1, s32[1,1024]{1,0:T(1,128)} %bitcast.14, s32[1]{0:T(128)S(6)} %copy.13.live_ref, s32[1,1024]{1,0:T(1,128)} %bitcast.15, f32[1,1024]{1,0:T(1,128)} %bitcast.16, f32[16,1024]{1,0:T(8,128)} %cov_hbm.1, ...), custom_call_target="tpu_custom_call" | custom-call | tf_op jit(solution)/shard_map/step/pallas_call | solution.py:614
  48.9 0.8 %finish.1 = (f32[32,768]{1,0:T(8,128)}, f32[64,1024]{1,0:T(8,128)}, f32[64,768]{1,0:T(8,128)}) custom-call(f32[32,768]{1,0:T(8,128)S(1)} %get-tuple-element.9.refs_0_, f32[64,1024]{1,0:T(8,128)S(1)} %get-tuple-element.10.refs_1_, f32[64,768]{1,0:T(8,128)S(1)} %get-tuple-element.11.refs_2_), custom_call_target="tpu_custom_call" | custom-call | tf_op jit(solution)/shard_map/finish/pallas_call | solution.py:677

commit v3 on v2

--- a/solution.py
+++ b/solution.py
@@ -266,13 +266,14 @@
 def all_kernel(
     n, m, counts_hbm, batch_hbm, live_ref, knot_hbm, frac_hbm, cov_hbm, coef_hbm, shift_hbm,
     factors_hbm, loads_hbm, beta_ref, fs_ref, ls_ref,
-    batch_ref, knot_ref, frac_ref, cov_ref, coef_ref, shift_ref, factors_ref, loads_ref,
+    batch_ref, knot_ref, frac_ref, cov_ref, factors_ref, loads_ref, p_own, p_all,
     counts, lin, rhs, pair_hi, pair_lo, tally, f_all, l_all, extra, tot_out, tot_in, known_c, known_f,
-    w_hi, w_lo, lhs_ref, g, g_pair, g_out, g_side, g_far, tall, turned, mine, theirs,
-    gl, l_pair, l_out, l_far, my_l, their_l, gf, z_in, z_relay, z_sum, my_f, their_f,
-    c_sem, i_sem, t_send, t_recv, gp_send, gp_recv, gs_send, gs_recv, gf_send, gf_recv,
-    b_send, b_recv, lp_send, lp_recv, lf_send, lf_recv, ol_send, ol_recv, z_send, z_recv,
-    of_send, of_recv,
+    cl_in, cl_own, cl_all, w_hi, w_lo, lhs_ref, g, g_pair, g_out, g_side, g_far, tall, turned, mine,
+    b_all, b_cat, gl, l_pair, l_out, l_far, my_l, their_l, gf,
+    c_sem, i_sem, t_send, t_recv, pz_send, pz_recv, px_send, px_recv, pp_send, pp_recv,
+    gp_send, gp_recv, gs_send, gs_recv, gf_send, gf_recv, ci_send, ci_recv, ca_send, ca_recv,
+    b_send, b_recv, bz_send, bz_recv, bx_send, bx_recv, bp_send, bp_recv,
+    lp_send, lp_recv, lf_send, lf_recv, ol_send, ol_recv,
 ):
     cell, gene = lax.axis_index("cell"), lax.axis_index("gene")
     core, chip = lax.rem(cell, 2), cell // 2
@@ -282,6 +283,9 @@
     rows = genes // n
     latent = loads_ref.shape[0]
     span = slots // m
+    width = SPL + cov_hbm.shape[0]
+    tall_p = p_own.shape[0]
+    coef_ref, shift_ref = p_own.at[0:width], p_own.at[width : width + BATCHES]
     arrive = meet_signal((("cell", n), ("gene", m)))
     loads_in = []
     for i in range(n):
@@ -306,6 +310,7 @@
     tot_out[...] = jnp.sum(part, axis=0, keepdims=True).astype(F32)
     for copy in small:
         copy.wait()
+    p_own[width + BATCHES :] = loads_ref[...].astype(F32)
     arrive()
     tot = []
     for d in range(1, m):
@@ -317,8 +322,42 @@
         )
         tot[-1].start()
 
+    line = gene // 2
+    near = gene + 1 - 2 * lax.rem(gene, 2)
+    others = [near, 2 - line, 3 - 3 * line]
+    beside, above = chip + 1 - 2 * lax.rem(chip, 2), lax.rem(chip + 2, chips)
+    places = [chips - 1 - chip, beside, above, chip]
+    partner = cell + 1 - 2 * core
+    deep, broad = tall_p // chips, genes // 2
+    p_rows = pl.ds(pl.multiple_of(chip * deep, deep), deep)
+    p_cols = pl.ds(pl.multiple_of(core * broad, broad), broad)
+    p_line = []
+    for i, z in enumerate(others):
+        p_line.append(
+            remote(
+                p_own.at[p_rows, p_cols], p_all.at[gene, p_rows, p_cols], pz_send.at[i],
+                pz_recv.at[gene], {"gene": z},
+            )
+        )
+        p_line[-1].start()
+
+    def p_landing(z):
+        piece = p_all.at[z, p_rows, p_cols]
+        return remote(piece, piece, pz_send.at[0], pz_recv.at[z], {"gene": near})
+
+    p_plane = {}
+
+    def p_forward(i):
+        z = others[i]
+        p_landing(z).wait_recv()
+        for k in range(chips - 1):
+            piece = p_all.at[z, p_rows, p_cols]
+            p_plane[i, k] = remote(
+                piece, piece, px_send.at[i, k], px_recv.at[i, k], {"cell": 2 * places[k] + core}
+            )
+            p_plane[i, k].start()
+
     hats, cov = design_of(knot_ref, frac_ref, cov_ref)
-    width = hats.shape[0] + cov.shape[0]
     design_hi, design_lo = split(jnp.concatenate([hats, cov], axis=0))
     hot = lax.broadcasted_iota(jnp.int32, (BATCHES, slots), 0) == batch_ref[...]
     hot = jnp.where(hot, 1.0, 0.0).astype(BF16)
@@ -348,9 +387,6 @@
         total = total + tot_in[d - 1]
     extra[0:1] = jnp.where(live, jnp.log((1.0 + total) / GENES), -1e30)
 
-    beside, above = chip + 1 - 2 * lax.rem(chip, 2), lax.rem(chip + 2, chips)
-    places = [chips - 1 - chip, beside, above, chip]
-    partner = cell + 1 - 2 * core
     wide = g.shape[3]
     cut = rows // 2
     upper, lower = slice(0, cut), slice(cut, rows)
@@ -376,6 +412,7 @@
         copy.start()
         return copy
 
+    p_forward(0)
     pair = [gram_chunk(0), gram_chunk(1)]
     pair[0].wait()
     g_out[0] = g[0, core] + g_pair[0]
@@ -402,13 +439,29 @@
     l_all[latent : 2 * latent] = l_hi
     l_all[2 * latent :] = l_lo
 
+    known_f[...] = mul(l_all[0:latent], counts[...].astype(F32).astype(BF16), ACROSS) * mask
+
+    def span_of(z):
+        return pl.ds(pl.multiple_of(z * span, span), span)
+
+    cl_line = []
+    for i, z in enumerate(others):
+        cl_line.append(
+            remote(
+                known_f.at[:, span_of(z)], cl_in.at[gene], ci_send.at[i], ci_recv.at[gene],
+                {"gene": z},
+            )
+        )
+        cl_line[-1].start()
+
     side[1].wait()
     g_out[1, lower] = g[1, core, lower] + g_pair[1, lower] + g_side[1]
     far.append(onward(1, lower, g_far.at[0, lower], gf_send.at[2], gf_recv.at[2], beside))
     side[0].wait()
     g_out[2, upper] = g[2, core, upper] + g_pair[2, upper] + g_side[0]
     far.append(onward(2, upper, g_far.at[1, upper], gf_send.at[3], gf_recv.at[3], above))
-    known_f[...] = mul(l_all[0:latent], counts[...].astype(F32).astype(BF16), ACROSS) * mask
+    p_forward(1)
+    p_forward(2)
     pair[3].wait()
     total = g[3, core] + g_pair[3]
     for copy in far:
@@ -423,53 +476,62 @@
     for d in range(1, n):
         out.append(
             remote(
-                mine, theirs.at[cell], b_send.at[d - 1], b_recv.at[d - 1],
+                mine, b_all.at[gene, core, chip], b_send.at[d - 1], b_recv.at[d - 1],
                 {"cell": lax.rem(cell + d, n)},
             )
         )
         out[-1].start()
-    theirs[cell] = mine[...]
-    for d in range(1, n):
-        out[d - 1].wait()
-    for o in range(n):
-        beta_ref[:, o * rows : (o + 1) * rows] = theirs[o, :, :rows]
-    beta_hi, beta_lo = split(beta_ref[...])
+    b_line = []
+    for i, z in enumerate(others):
+        b_line.append(
+            remote(
+                mine, b_all.at[gene, core, chip], bz_send.at[i], bz_recv.at[gene], {"gene": z}
+            )
+        )
+        b_line[-1].start()
+    b_all[gene, core, chip] = mine[...]
+
+    total = known_f[:, span_of(gene)]
+    for z in others:
+        remote(cl_in.at[z], cl_in.at[z], ci_send.at[0], ci_recv.at[z], {"gene": near}).wait_recv()
+        total = total + cl_in[z]
+    cl_own[...] = total
+    ca_line = []
+    for i, z in enumerate(others):
+        ca_line.append(
+            remote(cl_own, cl_all.at[gene], ca_send.at[i], ca_recv.at[gene], {"gene": z})
+        )
+        ca_line[-1].start()
+    cl_all[gene] = cl_own[...]
+
+    p_pair = []
+    for i, z in enumerate(others):
+        for k in range(chips - 1):
+            p_plane[i, k].wait()
+        half = p_all.at[z, :, p_cols]
+        p_pair.append(remote(half, half, pp_send.at[i], pp_recv.at[i], {"cell": partner}))
+        p_pair[-1].start()
+    for copy in out:
+        copy.wait()
+
+    def gather_betas(z):
+        for o in range(n):
+            b_cat[:, o * rows : (o + 1) * rows] = b_all[z, o % 2, o // 2, :, :rows]
+        return b_cat[...]
+
+    beta = gather_betas(gene)
+    beta_ref[...] = beta
+    beta_hi, beta_lo = split(beta)
     lhs_ref[...] = jnp.concatenate([beta_hi, beta_lo, beta_hi], axis=0).astype(F32).T.astype(BF16)
-
-    row = gene // 2
-    middle = lax.rem(gene + row, 2)
-    near = gene + 1 - 2 * lax.rem(gene, 2)
-    far_mid, far_end = 2 - row, 3 - 3 * row
-
-    def fact_chunk(j, owner):
-        cols = pl.ds(pl.multiple_of(owner * span, span), span)
-        delta = mul(lhs_ref[...], rhs[0 : 3 * width, cols], ACROSS)
-        high, low = split(jnp.exp(lin[:, cols] + delta))
-        w_hi[:, cols] = high
-        w_lo[:, cols] = low
-        first = mul(l_all[...], high, ACROSS)
-        second = mul(l_all[0 : 2 * latent], low, ACROSS)
-        gf[j, :latent] = known_f[:, cols] - first[:latent] - second[:latent]
-        gf[j, latent:] = first[latent : 2 * latent] + first[2 * latent :] + second[latent:]
-
-    def along(j, target, k, slot, place):
-        return remote(gf.at[j], target, z_send.at[k], z_recv.at[slot], {"gene": place})
-
-    relay = along(0, z_relay, 0, 3, near)
-    joined = along(0, z_in.at[1], 0, 1, far_mid)
-    straight = along(1, z_in.at[2 - middle], 1, 2 - middle, far_end)
-    close = along(2, z_in.at[0], 2, 0, near)
-    fact_chunk(0, far_mid)
-
-    @pl.when(middle == 0)
-    def _():
-        relay.start()
-
-    fact_chunk(1, far_end)
-    straight.start()
-    fact_chunk(2, near)
-    close.start()
-    fact_chunk(3, gene)
+    b_plane = {}
+    for i, z in enumerate(others):
+        piece = b_all.at[z, core, chip]
+        remote(piece, piece, bz_send.at[0], bz_recv.at[z], {"gene": near}).wait_recv()
+        for k in range(chips - 1):
+            b_plane[i, k] = remote(
+                piece, piece, bx_send.at[i, k], bx_recv.at[i, k], {"cell": 2 * places[k] + core}
+            )
+            b_plane[i, k].start()
 
     lpair, lfar = [], []
 
@@ -486,8 +548,12 @@
 
     for j in range(chips):
         at = pl.ds(pl.multiple_of(places[j] * block, block), block)
-        first = mul(w_hi[at], f_all[...], ROWS_BY_ROWS)
-        second = mul(w_lo[at], f_all[0 : 2 * latent], ROWS_BY_ROWS)
+        delta = mul(lhs_ref[at], rhs[0 : 3 * width], ACROSS)
+        high, low = split(jnp.exp(lin[at] + delta))
+        w_hi[at] = high
+        w_lo[at] = low
+        first = mul(high, f_all[...], ROWS_BY_ROWS)
+        second = mul(low, f_all[0 : 2 * latent], ROWS_BY_ROWS)
         grad = known_c[at, 2 * width :] - first[:, :latent] - second[:, :latent]
         curv = first[:, latent : 2 * latent] + first[:, 2 * latent :] + second[:, latent:]
         gl[j] = jnp.concatenate([grad, curv], axis=1).reshape(2, rows, 2 * latent)
@@ -498,12 +564,21 @@
         if j > 0:
             hand_on(j - 1)
 
-    @pl.when(middle == 1)
-    def _():
-        relay.wait_recv()
-        gf[0] = gf[0] + z_relay[...]
-        joined.start()
-
+    def gene_sums(loads, high, low):
+        first = mul(loads, high, ACROSS)
+        second = mul(loads[0 : 2 * latent], low, ACROSS)
+        grad = first[:latent] + second[:latent]
+        curv = first[latent : 2 * latent] + first[2 * latent :] + second[latent:]
+        return jnp.concatenate([grad, curv], axis=0)
+
+    gf[...] = gene_sums(l_all[...], w_hi[...], w_lo[...])
+    b_pair = []
+    for i, z in enumerate(others):
+        for k in range(chips - 1):
+            b_plane[i, k].wait()
+        half = b_all.at[z, core]
+        b_pair.append(remote(half, half, bp_send.at[i], bp_recv.at[i], {"cell": partner}))
+        b_pair[-1].start()
     lpair[-1].wait()
     total = gl[chips - 1, core] + l_pair[chips - 1]
     for j in range(chips - 1):
@@ -523,63 +598,28 @@
         )
         out_l[-1].start()
     their_l[cell] = my_l[...]
-
-    close.wait()
-    z_sum[...] = gf[3] + z_in[0]
-
-    @pl.when(middle == 0)
-    def _():
-        straight.wait()
-        z_sum[...] += z_in[2]
-        joined.wait_recv()
-        relay.wait_send()
-
-    @pl.when(middle == 1)
-    def _():
-        straight.wait_send()
-        joined.wait()
-
-    total = z_sum[...] + z_in[1]
-    my_f[...] = total[:latent] / (total[latent:] + 1.0)
-
-    def give(source, owner, k, place):
-        return remote(source, their_f.at[owner], of_send.at[k], of_recv.at[owner], {"gene": place})
-
-    give_a = give(my_f, gene, 0, far_end + middle * (far_mid - far_end))
-    give_b = give(my_f, gene, 1, far_mid + middle * (near - far_mid))
-    give_c = give(my_f, gene, 2, near)
-    pass_c = give(their_f.at[far_mid], far_mid, 2, near)
-    give_a.start()
-    give_b.start()
-
-    @pl.when(middle == 0)
-    def _():
-        give_c.start()
-
-    their_f[gene] = my_f[...]
-
-    @pl.when(middle == 1)
-    def _():
-        pass_c.wait_recv()
-        pass_c.start()
-
+    for i, z in enumerate(others):
+        p_pair[i].wait()
+        b_pair[i].wait()
+        next_hi, next_lo = split(p_all[z, 0:width] + gather_betas(z))
+        shift_hi, shift_lo = split(p_all[z, width : width + BATCHES])
+        wider = p_all[z, width + BATCHES :]
+        one = wider.astype(BF16)
+        two_hi, two_lo = split(wider * wider)
+        lhs = jnp.concatenate([next_hi, next_lo, next_hi, shift_hi, shift_lo, one], axis=0)
+        high, low = split(jnp.exp(mul(lhs, rhs[...], DOWN) + extra[0:1]))
+        gf[...] += gene_sums(jnp.concatenate([one, two_hi, two_lo], axis=0), high, low)
+    for z in others:
+        remote(cl_own, cl_all.at[z], ca_send.at[0], ca_recv.at[z], {"gene": near}).wait_recv()
+    for o in range(m):
+        at = slice(o * span, (o + 1) * span)
+        fs_ref[:, at] = (cl_all[o] - gf[:latent, at]) / (gf[latent:, at] + 1.0)
     for d in range(1, n):
         out_l[d - 1].wait()
     for o in range(n):
         ls_ref[:, o * rows : (o + 1) * rows] = their_l[o, :, :rows]
-
-    give(my_f, near, 0, near).wait_recv()
-    give(my_f, far_end, 0, near).wait_recv()
-
-    @pl.when(middle == 0)
-    def _():
-        pass_c.wait_recv()
-
-    give_a.wait_send()
-    give_b.wait_send()
-    give_c.wait_send()
-    for o in range(m):
-        fs_ref[:, o * span : (o + 1) * span] = their_f[o]
+    for copy in p_line + cl_line + ca_line + b_line:
+        copy.wait_send()
 
 
 def pass_on(*refs):
@@ -621,10 +661,10 @@
             vmem((1, slots), jnp.int32),
             vmem((1, slots), F32),
             vmem((ncov, slots), F32),
-            vmem((width, genes), F32),
-            vmem((BATCHES, genes), F32),
             vmem((latent, slots), BF16),
             vmem((latent, genes), BF16),
+            vmem((width + BATCHES + latent, genes), F32),
+            vmem((m, width + BATCHES + latent, genes), F32),
             vmem((genes, slots), jnp.int32),
             vmem((genes, slots), F32),
             vmem((3 * width + 2 * BATCHES + latent, slots), BF16),
@@ -638,6 +678,9 @@
             vmem((m - 1, 1, slots), F32),
             vmem((genes, 2 * width + latent), F32),
             vmem((latent, slots), F32),
+            vmem((m, latent, span), F32),
+            vmem((latent, span), F32),
+            vmem((m, latent, span), F32),
             vmem((genes, slots), BF16),
             vmem((genes, slots), BF16),
             vmem((genes, 3 * width), BF16),
@@ -649,24 +692,24 @@
             vmem((128, wide), F32),
             vmem((wide, 128), F32),
             vmem((width, 128), F32),
-            vmem((n, width, 128), F32),
+            vmem((m, 2, chips, width, 128), F32),
+            vmem((width, genes), F32),
             vmem((chips, 2, rows, 2 * latent), F32),
             vmem((chips, rows, 2 * latent), F32),
             vmem((chips - 1, rows, 2 * latent), F32),
             vmem((chips - 1, rows, 2 * latent), F32),
             vmem((latent, 128), F32),
             vmem((n, latent, 128), F32),
-            vmem((m, 2 * latent, span), F32),
-            vmem((m - 1, 2 * latent, span), F32),
-            vmem((2 * latent, span), F32),
-            vmem((2 * latent, span), F32),
-            vmem((latent, span), F32),
-            vmem((m, latent, span), F32),
+            vmem((2 * latent, slots), F32),
             dma((n,)), dma((8,)), dma((m - 1,)), dma((m - 1,)),
+            dma((m - 1,)), dma((m,)), dma((m - 1, chips - 1)), dma((m - 1, chips - 1)),
+            dma((m - 1,)), dma((m - 1,)),
             dma((chips,)), dma((chips,)), dma((2,)), dma((2,)), dma((4,)), dma((4,)),
+            dma((m - 1,)), dma((m,)), dma((m - 1,)), dma((m,)),
+            dma((n - 1,)), dma((n - 1,)), dma((m - 1,)), dma((m,)),
+            dma((m - 1, chips - 1)), dma((m - 1, chips - 1)), dma((m - 1,)), dma((m - 1,)),
+            dma((chips,)), dma((chips,)), dma((chips - 1,)), dma((chips - 1,)),
             dma((n - 1,)), dma((n - 1,)),
-            dma((chips,)), dma((chips,)), dma((chips - 1,)), dma((chips - 1,)),
-            dma((n - 1,)), dma((n - 1,)), dma((m - 1,)), dma((m,)), dma((m - 1,)), dma((m,)),
         ],
         compiler_params=params(collective_id=0, has_side_effects=True),
         name="step",
@@ -690,6 +733,8 @@
         and genes % (16 * n) == 0
         and genes // n <= 128
         and slots % (128 * m) == 0
+        and genes % 256 == 0
+        and (SPL + cov.shape[0] + BATCHES + factors.shape[1]) % 32 == 0
         and cov.shape[0] == SPL
         and factors.shape[1] == 64
     )

time: 49.9 us -> 45.9 us (0.920)
  Pallas kernels: 48.5 us -> 44.5 us
    pallas_call x1, Pallas kernels: 47.6 us -> 43.7 us  [local_fused(): pl.pallas_call(functools.partial(all_kernel, n, m), out_shape=shapes, in_...]
where the time goes in v3:
time: 45.9 us; the launch traced here: 45.8 us
  Pallas kernels  44.5 us (97%)
  between operations  1.29 us (3%)
    pallas_call x1, Pallas kernels, local_fused(): pl.pallas_call(functools.partial(all_kernel, n, m), out_shape=shapes, in_...  43.7 us

profile of v3, /device:TPU:0, one launch (start us, length us, event | category | flops | bytes accessed | tf_op | source)
XLA Modules:
  0.0 45.8 jit_solution(10034111673238792676)
XLA Ops:
  1.3 43.7 %step.1 = (f32[32,768]{1,0:T(8,128)S(1)}, f32[64,1024]{1,0:T(8,128)S(1)}, f32[64,768]{1,0:T(8,128)S(1)}) custom-call(s32[768,1024]{1,0:T(8,128)} %counts_hbm.1, s32[1,1024]{1,0:T(1,128)} %bitcast.14, s32[1]{0:T(128)S(6)} %copy.13.live_ref, s32[1,1024]{1,0:T(1,128)} %bitcast.15, f32[1,1024]{1,0:T(1,128)} %bitcast.16, f32[16,1024]{1,0:T(8,128)} %cov_hbm.1, ...), custom_call_target="tpu_custom_call" | custom-call | tf_op jit(solution)/shard_map/step/pallas_call | solution.py:654
  45.0 0.8 %finish.1 = (f32[32,768]{1,0:T(8,128)}, f32[64,1024]{1,0:T(8,128)}, f32[64,768]{1,0:T(8,128)}) custom-call(f32[32,768]{1,0:T(8,128)S(1)} %get-tuple-element.9.refs_0_, f32[64,1024]{1,0:T(8,128)S(1)} %get-tuple-element.10.refs_1_, f32[64,768]{1,0:T(8,128)S(1)} %get-tuple-element.11.refs_2_), custom_call_target="tpu_custom_call" | custom-call | tf_op jit(solution)/shard_map/finish/pallas_call | solution.py:720

commit v4 on v3

--- a/solution.py
+++ b/solution.py
@@ -263,13 +263,33 @@
         x[p : p + 1] = after
 
 
+def pack(block, full):
+    height, lanes = block.shape
+    kept = height * full // lanes
+    rest, part = block[kept:], lanes - full
+    found = [
+        pltpu.roll(rest, lanes - part - part * k, 1)[:, full:] for k in range(full // part)
+    ]
+    return jnp.concatenate([block[:kept, :full], jnp.concatenate(found, axis=0)], axis=1)
+
+
+def unpack(target, o, full, ref):
+    kept, lanes = ref.shape
+    part = lanes - full
+    more = kept * part // full
+    target[:kept, o * full : (o + 1) * full] = ref[:, :full]
+    for k in range(full // part):
+        at = o * full + k * part
+        target[kept:, at : at + part] = ref[k * more : (k + 1) * more, full:]
+
+
 def all_kernel(
     n, m, counts_hbm, batch_hbm, live_ref, knot_hbm, frac_hbm, cov_hbm, coef_hbm, shift_hbm,
     factors_hbm, loads_hbm, beta_ref, fs_ref, ls_ref,
     batch_ref, knot_ref, frac_ref, cov_ref, factors_ref, loads_ref, p_own, p_all,
     counts, lin, rhs, pair_hi, pair_lo, tally, f_all, l_all, extra, tot_out, tot_in, known_c, known_f,
     cl_in, cl_own, cl_all, w_hi, w_lo, lhs_ref, g, g_pair, g_out, g_side, g_far, tall, turned, mine,
-    b_all, b_cat, gl, l_pair, l_out, l_far, my_l, their_l, gf,
+    packed, b_all, b_cat, gl, l_pair, l_out, l_far, my_l, their_l, gf,
     c_sem, i_sem, t_send, t_recv, pz_send, pz_recv, px_send, px_recv, pp_send, pp_recv,
     gp_send, gp_recv, gs_send, gs_recv, gf_send, gf_recv, ci_send, ci_recv, ca_send, ca_recv,
     b_send, b_recv, bz_send, bz_recv, bx_send, bx_recv, bp_send, bp_recv,
@@ -322,40 +342,33 @@
         )
         tot[-1].start()
 
-    line = gene // 2
     near = gene + 1 - 2 * lax.rem(gene, 2)
-    others = [near, 2 - line, 3 - 3 * line]
+    others = [near, m - 1 - gene, lax.rem(gene + 2, m)]
     beside, above = chip + 1 - 2 * lax.rem(chip, 2), lax.rem(chip + 2, chips)
     places = [chips - 1 - chip, beside, above, chip]
     partner = cell + 1 - 2 * core
-    deep, broad = tall_p // chips, genes // 2
-    p_rows = pl.ds(pl.multiple_of(chip * deep, deep), deep)
+    deep, broad = tall_p // 2, genes // 2
     p_cols = pl.ds(pl.multiple_of(core * broad, broad), broad)
-    p_line = []
-    for i, z in enumerate(others):
-        p_line.append(
-            remote(
-                p_own.at[p_rows, p_cols], p_all.at[gene, p_rows, p_cols], pz_send.at[i],
-                pz_recv.at[gene], {"gene": z},
-            )
-        )
-        p_line[-1].start()
-
-    def p_landing(z):
-        piece = p_all.at[z, p_rows, p_cols]
-        return remote(piece, piece, pz_send.at[0], pz_recv.at[z], {"gene": near})
-
+    p_rows = [
+        pl.ds(0, tall_p),
+        pl.ds(pl.multiple_of(lax.rem(chip, 2) * deep, deep), deep),
+        pl.ds(pl.multiple_of(chip // 2 * deep, deep), deep),
+    ]
+    p_line = {}
+    for i in (1, 2, 0):
+        p_line[i] = remote(
+            p_own.at[p_rows[i], p_cols], p_all.at[gene, p_rows[i], p_cols], pz_send.at[i],
+            pz_recv.at[i], {"gene": others[i]},
+        )
     p_plane = {}
 
-    def p_forward(i):
-        z = others[i]
-        p_landing(z).wait_recv()
-        for k in range(chips - 1):
-            piece = p_all.at[z, p_rows, p_cols]
-            p_plane[i, k] = remote(
-                piece, piece, px_send.at[i, k], px_recv.at[i, k], {"cell": 2 * places[k] + core}
-            )
-            p_plane[i, k].start()
+    def p_forward(i, place):
+        p_line[i].wait()
+        piece = p_all.at[others[i], p_rows[i], p_cols]
+        p_plane[i] = remote(
+            piece, piece, px_send.at[i - 1], px_recv.at[i - 1], {"cell": 2 * place + core}
+        )
+        p_plane[i].start()
 
     hats, cov = design_of(knot_ref, frac_ref, cov_ref)
     design_hi, design_lo = split(jnp.concatenate([hats, cov], axis=0))
@@ -386,6 +399,8 @@
         tot[d - 1].wait()
         total = total + tot_in[d - 1]
     extra[0:1] = jnp.where(live, jnp.log((1.0 + total) / GENES), -1e30)
+    for i in (1, 2, 0):
+        p_line[i].start()
 
     wide = g.shape[3]
     cut = rows // 2
@@ -412,7 +427,6 @@
         copy.start()
         return copy
 
-    p_forward(0)
     pair = [gram_chunk(0), gram_chunk(1)]
     pair[0].wait()
     g_out[0] = g[0, core] + g_pair[0]
@@ -460,8 +474,6 @@
     side[0].wait()
     g_out[2, upper] = g[2, core, upper] + g_pair[2, upper] + g_side[0]
     far.append(onward(2, upper, g_far.at[1, upper], gf_send.at[3], gf_recv.at[3], above))
-    p_forward(1)
-    p_forward(2)
     pair[3].wait()
     total = g[3, core] + g_pair[3]
     for copy in far:
@@ -472,66 +484,61 @@
         tall[rows:128] = jnp.zeros((128 - rows, wide), F32)
     turned[...] = tall[...].T
     solve(turned, mine)
+    packed[...] = pack(mine[...], rows)
+    b_line = []
+    for i, z in enumerate(others):
+        b_line.append(
+            remote(packed, b_all.at[gene, core, chip], bz_send.at[i], bz_recv.at[i], {"gene": z})
+        )
+        b_line[-1].start()
     out = []
     for d in range(1, n):
         out.append(
             remote(
-                mine, b_all.at[gene, core, chip], b_send.at[d - 1], b_recv.at[d - 1],
+                packed, b_all.at[gene, core, chip], b_send.at[d - 1], b_recv.at[d - 1],
                 {"cell": lax.rem(cell + d, n)},
             )
         )
         out[-1].start()
-    b_line = []
-    for i, z in enumerate(others):
-        b_line.append(
-            remote(
-                mine, b_all.at[gene, core, chip], bz_send.at[i], bz_recv.at[gene], {"gene": z}
-            )
-        )
-        b_line[-1].start()
-    b_all[gene, core, chip] = mine[...]
-
-    total = known_f[:, span_of(gene)]
-    for z in others:
-        remote(cl_in.at[z], cl_in.at[z], ci_send.at[0], ci_recv.at[z], {"gene": near}).wait_recv()
-        total = total + cl_in[z]
-    cl_own[...] = total
-    ca_line = []
-    for i, z in enumerate(others):
-        ca_line.append(
-            remote(cl_own, cl_all.at[gene], ca_send.at[i], ca_recv.at[gene], {"gene": z})
-        )
-        ca_line[-1].start()
-    cl_all[gene] = cl_own[...]
-
-    p_pair = []
-    for i, z in enumerate(others):
-        for k in range(chips - 1):
-            p_plane[i, k].wait()
-        half = p_all.at[z, :, p_cols]
-        p_pair.append(remote(half, half, pp_send.at[i], pp_recv.at[i], {"cell": partner}))
-        p_pair[-1].start()
-    for copy in out:
-        copy.wait()
-
-    def gather_betas(z):
-        for o in range(n):
-            b_cat[:, o * rows : (o + 1) * rows] = b_all[z, o % 2, o // 2, :, :rows]
-        return b_cat[...]
-
-    beta = gather_betas(gene)
-    beta_ref[...] = beta
-    beta_hi, beta_lo = split(beta)
-    lhs_ref[...] = jnp.concatenate([beta_hi, beta_lo, beta_hi], axis=0).astype(F32).T.astype(BF16)
+    b_all[gene, core, chip] = packed[...]
+
     b_plane = {}
-    for i, z in enumerate(others):
-        piece = b_all.at[z, core, chip]
-        remote(piece, piece, bz_send.at[0], bz_recv.at[z], {"gene": near}).wait_recv()
+
+    def b_forward(i):
+        b_line[i].wait()
+        piece = b_all.at[others[i], core, chip]
         for k in range(chips - 1):
             b_plane[i, k] = remote(
                 piece, piece, bx_send.at[i, k], bx_recv.at[i, k], {"cell": 2 * places[k] + core}
             )
             b_plane[i, k].start()
+
+    b_pair = []
+
+    def b_swap(i):
+        for k in range(chips - 1):
+            b_plane[i, k].wait()
+        half = b_all.at[others[i], core]
+        b_pair.append(remote(half, half, bp_send.at[i], bp_recv.at[i], {"cell": partner}))
+        b_pair[-1].start()
+
+    b_forward(0)
+    p_forward(1, beside)
+    p_forward(2, above)
+    for copy in out:
+        copy.wait()
+
+    def gather_betas(z):
+        for o in range(n):
+            unpack(b_cat, o, rows, b_all.at[z, o % 2, o // 2])
+        return b_cat[...]
+
+    beta = gather_betas(gene)
+    beta_ref[...] = beta
+    beta_hi, beta_lo = split(beta)
+    lhs_ref[...] = jnp.concatenate([beta_hi, beta_lo, beta_hi], axis=0).astype(F32).T.astype(BF16)
+    b_forward(1)
+    b_forward(2)
 
     lpair, lfar = [], []
 
@@ -571,34 +578,19 @@
         curv = first[latent : 2 * latent] + first[2 * latent :] + second[latent:]
         return jnp.concatenate([grad, curv], axis=0)
 
+    p_pair = []
+    p_line[0].wait()
+    p_plane[1].wait()
+    p_plane[2].wait()
+    for i, z in enumerate(others):
+        half = p_all.at[z, :, p_cols]
+        p_pair.append(remote(half, half, pp_send.at[i], pp_recv.at[i], {"cell": partner}))
+        p_pair[-1].start()
+    b_swap(0)
     gf[...] = gene_sums(l_all[...], w_hi[...], w_lo[...])
-    b_pair = []
-    for i, z in enumerate(others):
-        for k in range(chips - 1):
-            b_plane[i, k].wait()
-        half = b_all.at[z, core]
-        b_pair.append(remote(half, half, bp_send.at[i], bp_recv.at[i], {"cell": partner}))
-        b_pair[-1].start()
-    lpair[-1].wait()
-    total = gl[chips - 1, core] + l_pair[chips - 1]
-    for j in range(chips - 1):
-        lfar[j].wait()
-        total = total + l_far[j]
-    if rows < 128:
-        total = jnp.concatenate([total, jnp.zeros((128 - rows, 2 * latent), F32)], axis=0)
-    total = total.T
-    my_l[...] = total[:latent] / jnp.sqrt(total[latent:] + 1.0)
-    out_l = []
-    for d in range(1, n):
-        out_l.append(
-            remote(
-                my_l, their_l.at[cell], ol_send.at[d - 1], ol_recv.at[d - 1],
-                {"cell": lax.rem(cell + d, n)},
-            )
-        )
-        out_l[-1].start()
-    their_l[cell] = my_l[...]
-    for i, z in enumerate(others):
+
+    def other_genes(i):
+        z = others[i]
         p_pair[i].wait()
         b_pair[i].wait()
         next_hi, next_lo = split(p_all[z, 0:width] + gather_betas(z))
@@ -609,6 +601,44 @@
         lhs = jnp.concatenate([next_hi, next_lo, next_hi, shift_hi, shift_lo, one], axis=0)
         high, low = split(jnp.exp(mul(lhs, rhs[...], DOWN) + extra[0:1]))
         gf[...] += gene_sums(jnp.concatenate([one, two_hi, two_lo], axis=0), high, low)
+
+    total = known_f[:, span_of(gene)]
+    for z in others:
+        remote(cl_in.at[z], cl_in.at[z], ci_send.at[0], ci_recv.at[z], {"gene": near}).wait_recv()
+        total = total + cl_in[z]
+    cl_own[...] = total
+    ca_line = []
+    for i, z in enumerate(others):
+        ca_line.append(
+            remote(cl_own, cl_all.at[gene], ca_send.at[i], ca_recv.at[gene], {"gene": z})
+        )
+        ca_line[-1].start()
+    cl_all[gene] = cl_own[...]
+
+    lpair[-1].wait()
+    total = gl[chips - 1, core] + l_pair[chips - 1]
+    b_swap(1)
+    b_swap(2)
+    other_genes(0)
+    for j in range(chips - 1):
+        lfar[j].wait()
+        total = total + l_far[j]
+    if rows < 128:
+        total = jnp.concatenate([total, jnp.zeros((128 - rows, 2 * latent), F32)], axis=0)
+    total = total.T
+    my_l[...] = pack(total[:latent] / jnp.sqrt(total[latent:] + 1.0), rows)
+    out_l = []
+    for d in range(1, n):
+        out_l.append(
+            remote(
+                my_l, their_l.at[cell], ol_send.at[d - 1], ol_recv.at[d - 1],
+                {"cell": lax.rem(cell + d, n)},
+            )
+        )
+        out_l[-1].start()
+    their_l[cell] = my_l[...]
+    other_genes(1)
+    other_genes(2)
     for z in others:
         remote(cl_own, cl_all.at[z], ca_send.at[0], ca_recv.at[z], {"gene": near}).wait_recv()
     for o in range(m):
@@ -617,8 +647,8 @@
     for d in range(1, n):
         out_l[d - 1].wait()
     for o in range(n):
-        ls_ref[:, o * rows : (o + 1) * rows] = their_l[o, :, :rows]
-    for copy in p_line + cl_line + ca_line + b_line:
+        unpack(ls_ref, o, rows, their_l.at[o])
+    for copy in cl_line + ca_line:
         copy.wait_send()
 
 
@@ -692,21 +722,22 @@
             vmem((128, wide), F32),
             vmem((wide, 128), F32),
             vmem((width, 128), F32),
-            vmem((m, 2, chips, width, 128), F32),
+            vmem((width * rows // 128, 128), F32),
+            vmem((m, 2, chips, width * rows // 128, 128), F32),
             vmem((width, genes), F32),
             vmem((chips, 2, rows, 2 * latent), F32),
             vmem((chips, rows, 2 * latent), F32),
             vmem((chips - 1, rows, 2 * latent), F32),
             vmem((chips - 1, rows, 2 * latent), F32),
-            vmem((latent, 128), F32),
-            vmem((n, latent, 128), F32),
+            vmem((latent * rows // 128, 128), F32),
+            vmem((n, latent * rows // 128, 128), F32),
             vmem((2 * latent, slots), F32),
             dma((n,)), dma((8,)), dma((m - 1,)), dma((m - 1,)),
-            dma((m - 1,)), dma((m,)), dma((m - 1, chips - 1)), dma((m - 1, chips - 1)),
+            dma((m - 1,)), dma((m - 1,)), dma((2,)), dma((2,)),
             dma((m - 1,)), dma((m - 1,)),
             dma((chips,)), dma((chips,)), dma((2,)), dma((2,)), dma((4,)), dma((4,)),
             dma((m - 1,)), dma((m,)), dma((m - 1,)), dma((m,)),
-            dma((n - 1,)), dma((n - 1,)), dma((m - 1,)), dma((m,)),
+            dma((n - 1,)), dma((n - 1,)), dma((m - 1,)), dma((m - 1,)),
             dma((m - 1, chips - 1)), dma((m - 1, chips - 1)), dma((m - 1,)), dma((m - 1,)),
             dma((chips,)), dma((chips,)), dma((chips - 1,)), dma((chips - 1,)),
             dma((n - 1,)), dma((n - 1,)),
@@ -731,10 +762,10 @@
         n == 8
         and m == 4
         and genes % (16 * n) == 0
-        and genes // n <= 128
+        and genes // n == 96
         and slots % (128 * m) == 0
         and genes % 256 == 0
-        and (SPL + cov.shape[0] + BATCHES + factors.shape[1]) % 32 == 0
+        and (SPL + cov.shape[0] + BATCHES + factors.shape[1]) % 16 == 0
         and cov.shape[0] == SPL
         and factors.shape[1] == 64
     )

time: 45.9 us -> 43 us (0.937)
  Pallas kernels: 44.5 us -> 41.5 us
    pallas_call x1, Pallas kernels: 43.7 us -> 40.7 us  [local_fused(): pl.pallas_call(functools.partial(all_kernel, n, m), out_shape=shapes, in_...]
where the time goes in v4:
time: 43 us; the launch traced here: 42.8 us
  Pallas kernels  41.5 us (97%)
  between operations  1.29 us (3%)
    pallas_call x1, Pallas kernels, local_fused(): pl.pallas_call(functools.partial(all_kernel, n, m), out_shape=shapes, in_...  40.7 us

profile of v4, /device:TPU:0, one launch (start us, length us, event | category | flops | bytes accessed | tf_op | source)
XLA Modules:
  0.0 42.8 jit_solution(1577451777051752960)
XLA Ops:
  1.3 40.7 %step.1 = (f32[32,768]{1,0:T(8,128)S(1)}, f32[64,1024]{1,0:T(8,128)S(1)}, f32[64,768]{1,0:T(8,128)S(1)}) custom-call(s32[768,1024]{1,0:T(8,128)} %counts_hbm.1, s32[1,1024]{1,0:T(1,128)} %bitcast.14, s32[1]{0:T(128)S(6)} %copy.13.live_ref, s32[1,1024]{1,0:T(1,128)} %bitcast.15, f32[1,1024]{1,0:T(1,128)} %bitcast.16, f32[16,1024]{1,0:T(8,128)} %cov_hbm.1, ...), custom_call_target="tpu_custom_call" | custom-call | tf_op jit(solution)/shard_map/step/pallas_call | solution.py:684
  42.0 0.8 %finish.1 = (f32[32,768]{1,0:T(8,128)}, f32[64,1024]{1,0:T(8,128)}, f32[64,768]{1,0:T(8,128)}) custom-call(f32[32,768]{1,0:T(8,128)S(1)} %get-tuple-element.9.refs_0_, f32[64,1024]{1,0:T(8,128)S(1)} %get-tuple-element.10.refs_1_, f32[64,768]{1,0:T(8,128)S(1)} %get-tuple-element.11.refs_2_), custom_call_target="tpu_custom_call" | custom-call | tf_op jit(solution)/shard_map/finish/pallas_call | solution.py:751

commit v5 on v4

--- a/solution.py
+++ b/solution.py
@@ -288,7 +288,7 @@
     factors_hbm, loads_hbm, beta_ref, fs_ref, ls_ref,
     batch_ref, knot_ref, frac_ref, cov_ref, factors_ref, loads_ref, p_own, p_all,
     counts, lin, rhs, pair_hi, pair_lo, tally, f_all, l_all, extra, tot_out, tot_in, known_c, known_f,
-    cl_in, cl_own, cl_all, w_hi, w_lo, lhs_ref, g, g_pair, g_out, g_side, g_far, tall, turned, mine,
+    cl_in, cl_relay, cl_out, cl_own, cl_all, w_hi, w_lo, lhs_ref, g, g_pair, g_out, g_side, g_far, tall, turned, mine,
     packed, b_all, b_cat, gl, l_pair, l_out, l_far, my_l, their_l, gf,
     c_sem, i_sem, t_send, t_recv, pz_send, pz_recv, px_send, px_recv, pp_send, pp_recv,
     gp_send, gp_recv, gs_send, gs_recv, gf_send, gf_recv, ci_send, ci_recv, ca_send, ca_recv,
@@ -360,6 +360,7 @@
             p_own.at[p_rows[i], p_cols], p_all.at[gene, p_rows[i], p_cols], pz_send.at[i],
             pz_recv.at[i], {"gene": others[i]},
         )
+    p_line[0].start()
     p_plane = {}
 
     def p_forward(i, place):
@@ -399,7 +400,7 @@
         tot[d - 1].wait()
         total = total + tot_in[d - 1]
     extra[0:1] = jnp.where(live, jnp.log((1.0 + total) / GENES), -1e30)
-    for i in (1, 2, 0):
+    for i in (1, 2):
         p_line[i].start()
 
     wide = g.shape[3]
@@ -458,15 +459,28 @@
     def span_of(z):
         return pl.ds(pl.multiple_of(z * span, span), span)
 
-    cl_line = []
-    for i, z in enumerate(others):
-        cl_line.append(
-            remote(
-                known_f.at[:, span_of(z)], cl_in.at[gene], ci_send.at[i], ci_recv.at[gene],
-                {"gene": z},
-            )
-        )
-        cl_line[-1].start()
+    row = gene // 2
+    middle = lax.rem(gene + row, 2)
+    far_mid, far_end = 2 - row, 3 - 3 * row
+
+    def cl_copy(source, target, k, slot, place):
+        return remote(source, target, ci_send.at[k], ci_recv.at[slot], {"gene": place})
+
+    cl_ahead = [
+        cl_copy(known_f.at[:, span_of(z)], cl_relay.at[k], k, 2 + k, near)
+        for k, z in enumerate((far_mid, far_end))
+    ]
+    cl_joined = [
+        cl_copy(cl_out.at[k], cl_in.at[1], k, 1, z) for k, z in enumerate((far_mid, far_end))
+    ]
+    cl_close = cl_copy(known_f.at[:, span_of(near)], cl_in.at[0], 2, 0, near)
+
+    @pl.when(middle == 0)
+    def _():
+        cl_ahead[0].start()
+        cl_ahead[1].start()
+
+    cl_close.start()
 
     side[1].wait()
     g_out[1, lower] = g[1, core, lower] + g_pair[1, lower] + g_side[1]
@@ -476,6 +490,14 @@
     far.append(onward(2, upper, g_far.at[1, upper], gf_send.at[3], gf_recv.at[3], above))
     pair[3].wait()
     total = g[3, core] + g_pair[3]
+
+    @pl.when(middle == 1)
+    def _():
+        for k, z in enumerate((far_mid, far_end)):
+            cl_ahead[k].wait_recv()
+            cl_out[k] = known_f[:, span_of(z)] + cl_relay[k]
+            cl_joined[k].start()
+
     for copy in far:
         copy.wait()
     total = total + g_far[0] + g_far[1]
@@ -523,6 +545,15 @@
         b_pair[-1].start()
 
     b_forward(0)
+    p_pair = []
+
+    def p_swap(i):
+        half = p_all.at[others[i], :, p_cols]
+        p_pair.append(remote(half, half, pp_send.at[i], pp_recv.at[i], {"cell": partner}))
+        p_pair[-1].start()
+
+    p_line[0].wait()
+    p_swap(0)
     p_forward(1, beside)
     p_forward(2, above)
     for copy in out:
@@ -570,6 +601,8 @@
         lpair[-1].start()
         if j > 0:
             hand_on(j - 1)
+        if j == 1:
+            b_swap(0)
 
     def gene_sums(loads, high, low):
         first = mul(loads, high, ACROSS)
@@ -578,15 +611,9 @@
         curv = first[latent : 2 * latent] + first[2 * latent :] + second[latent:]
         return jnp.concatenate([grad, curv], axis=0)
 
-    p_pair = []
-    p_line[0].wait()
-    p_plane[1].wait()
-    p_plane[2].wait()
-    for i, z in enumerate(others):
-        half = p_all.at[z, :, p_cols]
-        p_pair.append(remote(half, half, pp_send.at[i], pp_recv.at[i], {"cell": partner}))
-        p_pair[-1].start()
-    b_swap(0)
+    for i in (1, 2):
+        p_plane[i].wait()
+        p_swap(i)
     gf[...] = gene_sums(l_all[...], w_hi[...], w_lo[...])
 
     def other_genes(i):
@@ -602,11 +629,11 @@
         high, low = split(jnp.exp(mul(lhs, rhs[...], DOWN) + extra[0:1]))
         gf[...] += gene_sums(jnp.concatenate([one, two_hi, two_lo], axis=0), high, low)
 
-    total = known_f[:, span_of(gene)]
-    for z in others:
-        remote(cl_in.at[z], cl_in.at[z], ci_send.at[0], ci_recv.at[z], {"gene": near}).wait_recv()
-        total = total + cl_in[z]
-    cl_own[...] = total
+    cl_close.wait()
+    cl_joined[0].wait_recv()
+    cl_joined[0].wait_send()
+    cl_joined[1].wait_send()
+    cl_own[...] = known_f[:, span_of(gene)] + cl_in[0] + cl_in[1]
     ca_line = []
     for i, z in enumerate(others):
         ca_line.append(
@@ -648,7 +675,7 @@
         out_l[d - 1].wait()
     for o in range(n):
         unpack(ls_ref, o, rows, their_l.at[o])
-    for copy in cl_line + ca_line:
+    for copy in ca_line:
         copy.wait_send()
 
 
@@ -708,7 +735,9 @@
             vmem((m - 1, 1, slots), F32),
             vmem((genes, 2 * width + latent), F32),
             vmem((latent, slots), F32),
-            vmem((m, latent, span), F32),
+            vmem((2, latent, span), F32),
+            vmem((2, latent, span), F32),
+            vmem((2, latent, span), F32),
             vmem((latent, span), F32),
             vmem((m, latent, span), F32),
             vmem((genes, slots), BF16),

time: 43 us -> 41.4 us (0.963)
  Pallas kernels: 41.5 us -> 39.9 us
    pallas_call x1, Pallas kernels: 40.7 us -> 39.1 us  [local_fused(): pl.pallas_call(functools.partial(all_kernel, n, m), out_shape=shapes, in_...]
where the time goes in v5:
time: 41.4 us; the launch traced here: 41.2 us
  Pallas kernels  39.9 us (96%)
  between operations  1.29 us (3%)
    pallas_call x1, Pallas kernels, local_fused(): pl.pallas_call(functools.partial(all_kernel, n, m), out_shape=shapes, in_...  39.1 us
    pallas_call x1, Pallas kernels, local_fused(): pl.pallas_call(pass_on, out_shape=shapes, in_specs=[VM] * 3, out_specs=(V...  0.83 us

profile of v5, /device:TPU:0, one launch (start us, length us, event | category | flops | bytes accessed | tf_op | source)
XLA Modules:
  0.0 41.2 jit_solution(15299089909859827671)
XLA Ops:
  1.3 39.1 %step.1 = (f32[32,768]{1,0:T(8,128)S(1)}, f32[64,1024]{1,0:T(8,128)S(1)}, f32[64,768]{1,0:T(8,128)S(1)}) custom-call(s32[768,1024]{1,0:T(8,128)} %counts_hbm.1, s32[1,1024]{1,0:T(1,128)} %bitcast.14, s32[1]{0:T(128)S(6)} %copy.13.live_ref, s32[1,1024]{1,0:T(1,128)} %bitcast.15, f32[1,1024]{1,0:T(1,128)} %bitcast.16, f32[16,1024]{1,0:T(8,128)} %cov_hbm.1, ...), custom_call_target="tpu_custom_call" | custom-call | tf_op jit(solution)/shard_map/step/pallas_call | solution.py:711
  40.4 0.8 %finish.1 = (f32[32,768]{1,0:T(8,128)}, f32[64,1024]{1,0:T(8,128)}, f32[64,768]{1,0:T(8,128)}) custom-call(f32[32,768]{1,0:T(8,128)S(1)} %get-tuple-element.9.refs_0_, f32[64,1024]{1,0:T(8,128)S(1)} %get-tuple-element.10.refs_1_, f32[64,768]{1,0:T(8,128)S(1)} %get-tuple-element.11.refs_2_), custom_call_target="tpu_custom_call" | custom-call | tf_op jit(solution)/shard_map/finish/pallas_call | solution.py:780

commit v6 on v5

--- a/solution.py
+++ b/solution.py
@@ -507,12 +507,6 @@
     turned[...] = tall[...].T
     solve(turned, mine)
     packed[...] = pack(mine[...], rows)
-    b_line = []
-    for i, z in enumerate(others):
-        b_line.append(
-            remote(packed, b_all.at[gene, core, chip], bz_send.at[i], bz_recv.at[i], {"gene": z})
-        )
-        b_line[-1].start()
     out = []
     for d in range(1, n):
         out.append(
@@ -522,6 +516,12 @@
             )
         )
         out[-1].start()
+    b_line = []
+    for i, z in enumerate(others):
+        b_line.append(
+            remote(packed, b_all.at[gene, core, chip], bz_send.at[i], bz_recv.at[i], {"gene": z})
+        )
+        b_line[-1].start()
     b_all[gene, core, chip] = packed[...]
 
     b_plane = {}
@@ -568,8 +568,6 @@
     beta_ref[...] = beta
     beta_hi, beta_lo = split(beta)
     lhs_ref[...] = jnp.concatenate([beta_hi, beta_lo, beta_hi], axis=0).astype(F32).T.astype(BF16)
-    b_forward(1)
-    b_forward(2)
 
     lpair, lfar = [], []
 
@@ -601,6 +599,9 @@
         lpair[-1].start()
         if j > 0:
             hand_on(j - 1)
+        if j == 0:
+            b_forward(1)
+            b_forward(2)
         if j == 1:
             b_swap(0)
 

time: 41.4 us -> 41.4 us (level)
  no operation moved by 1% of the time
where the time goes in v6:
time: 41.4 us; the launch traced here: 41.2 us
  Pallas kernels  39.9 us (96%)
  between operations  1.29 us (3%)
    pallas_call x1, Pallas kernels, local_fused(): pl.pallas_call(functools.partial(all_kernel, n, m), out_shape=shapes, in_...  39.1 us
    pallas_call x1, Pallas kernels, local_fused(): pl.pallas_call(pass_on, out_shape=shapes, in_specs=[VM] * 3, out_specs=(V...  0.83 us

profile of v6, /device:TPU:0, one launch (start us, length us, event | category | flops | bytes accessed | tf_op | source)
XLA Modules:
  0.0 41.2 jit_solution(7294220354153666974)
XLA Ops:
  1.3 39.1 %step.1 = (f32[32,768]{1,0:T(8,128)S(1)}, f32[64,1024]{1,0:T(8,128)S(1)}, f32[64,768]{1,0:T(8,128)S(1)}) custom-call(s32[768,1024]{1,0:T(8,128)} %counts_hbm.1, s32[1,1024]{1,0:T(1,128)} %bitcast.14, s32[1]{0:T(128)S(6)} %copy.13.live_ref, s32[1,1024]{1,0:T(1,128)} %bitcast.15, f32[1,1024]{1,0:T(1,128)} %bitcast.16, f32[16,1024]{1,0:T(8,128)} %cov_hbm.1, ...), custom_call_target="tpu_custom_call" | custom-call | tf_op jit(solution)/shard_map/step/pallas_call | solution.py:712
  40.4 0.8 %finish.1 = (f32[32,768]{1,0:T(8,128)}, f32[64,1024]{1,0:T(8,128)}, f32[64,768]{1,0:T(8,128)}) custom-call(f32[32,768]{1,0:T(8,128)S(1)} %get-tuple-element.9.refs_0_, f32[64,1024]{1,0:T(8,128)S(1)} %get-tuple-element.10.refs_1_, f32[64,768]{1,0:T(8,128)S(1)} %get-tuple-element.11.refs_2_), custom_call_target="tpu_custom_call" | custom-call | tf_op jit(solution)/shard_map/finish/pallas_call | solution.py:781
